TPU v7x, 256 devices: a whole 4x4x8 slice. The times are simulated.
256 devices in a mesh: batch: 32 (over z, y), dim: 8 (over x, core).
Axes of the slice: x: 4, y: 4, z: 8, core: 2. Of those that a mesh axis runs over, the one named last changes fastest.
Arguments:
- x_start: float32 [1024], P('dim'), may hold values from 0.5 to 2
- y_start: float32 [], replicated, may hold values from -1 to 1
- z_start: float32 [1024], P('dim'), may hold values from -3 to 3
- increments: float32 [5, 8192, 1024], P(None, 'batch', 'dim'), may hold values from -2.7 to 2.7
- default_step: int32 [8192], P('batch'), may hold values from 0 to 6
- term_weight: float32 [1024], P('dim'), may hold values from -6 to 6
- w_first: bfloat16 [4, 1024, 1024], P(None, None, 'dim'), may hold values from -0.1875 to 0.1875
- w_second: bfloat16 [4, 1024, 1024], P(None, 'dim'), may hold values from -0.1875 to 0.1875
- w_third: bfloat16 [4, 1024, 1024], P(None, None, 'dim'), may hold values from -0.1875 to 0.1875
Outputs:
- loss: float32 [], replicated
- grad_y: float32 [], replicated
- grad_z: float32 [1024], P('dim')
- grad_first: bfloat16 [4, 1024, 1024], P(None, None, 'dim')
- grad_second: bfloat16 [4, 1024, 1024], P(None, 'dim')
- grad_third: bfloat16 [4, 1024, 1024], P(None, None, 'dim')
Inputs may be any that keep to these rules, and one draw needn't show every extreme that they name: `default_step`: the time step at which a path defaults; 5 or more means no default within the window.
All inputs are finite; a program needn't handle non-finite values.
Results may differ from a plain program's by a relative error of at most 0.0085.
Values may be sent and summed in bfloat16 or wider, within the bound.
No kernel may reach another device: no remote copies, remote signals or barrier semaphores. Data moves between devices by JAX's collectives and lax.ppermute only.
A program may use at most 64 MiB of HBM per device.

v0:
```python
import math

import jax
import jax.numpy as jnp
from jax import lax
from jax.experimental import pallas as pl
from jax.experimental.pallas import tpu as pltpu
from jax.sharding import Mesh
from jax.sharding import PartitionSpec as P


D = 1024

DRIFT_RATE = 0.06
VOLATILITY = 0.2
DISCOUNT = 0.02
DEFAULT_LOSS = 1.0 / 3.0

X, CORES, Y, Z = 4, 2, 4, 8
W = D // (X * CORES)
BF = jnp.bfloat16
F32 = jnp.float32


def shifted(value, axis, n, o):
    return lax.ppermute(value, axis, [(i, (i + o) % n) for i in range(n)])


def flipped(value, axis, n, bit):
    return lax.ppermute(value, axis, [(i, i ^ bit) for i in range(n)])


def x_plus(value, o):
    return shifted(value, "x", X, o)


def y_plus(value, o):
    return shifted(value, "y", Y, o)


def z_plus(value, o):
    return shifted(value, "z", Z, o)


def turned(value):
    pairs = [(X * y + x, X * x + y) for y in range(Y) for x in range(X)]
    return lax.ppermute(value, ("y", "x"), pairs)


def core_swap(value):
    return flipped(value, "core", CORES, 1)


def pick(array, index):
    return lax.dynamic_index_in_dim(array, index, 0, keepdims=False)


def dot(a, b, contract):
    return lax.dot_general(a, b, (contract, ((), ())), preferred_element_type=F32)


def vmem_call(kernel, place, args, outs, scratch=()):
    vmem = pl.BlockSpec(memory_space=pltpu.VMEM)
    return pl.pallas_call(
        kernel,
        out_shape=[jax.ShapeDtypeStruct(shape, dtype) for shape, dtype in outs],
        in_specs=[pl.BlockSpec(memory_space=pltpu.SMEM)] + [vmem] * len(args),
        out_specs=[vmem] * len(outs),
        scratch_shapes=list(scratch),
    )(place, *args)


def two_words(value):
    high = value.astype(BF).astype(F32)
    return jnp.concatenate([high, value - high], axis=0).astype(BF)


def arrange_kernel(place, near, far, inputs, incs):
    x, c = place[0], place[1]
    for i in range(X):
        r = lax.rem(x + (X - i), X)
        inputs[:, pl.ds(pl.multiple_of(2 * W * i + W * c, W), W)] = near[r, 0]
        inputs[:, pl.ds(pl.multiple_of(2 * W * i + W * (1 - c), W), W)] = far[r, 0]
        incs[:, 2 * W * i : 2 * W * i + W] = near[i, 1]
        incs[:, 2 * W * i + W : 2 * W * i + 2 * W] = far[i, 1]


def pack_kernel(place, first, second, third, far, out, sems):
    c, y = place[1], place[2]
    half = far.shape[0]
    copies = [
        (first.at[y], out.at[:D, :]),
        (third.at[y, c], out.at[2 * D : 2 * D + half, :]),
        (far, out.at[2 * D + half :, :]),
    ]
    for k in range(D // W):
        copies.append((second.at[y, :, pl.ds(W * k, W)], out.at[D + W * k : D + W * k + W, :]))
    copies = [pltpu.make_async_copy(a, b, sems.at[i]) for i, (a, b) in enumerate(copies)]
    for copy in copies:
        copy.start()
    for copy in copies:
        copy.wait()


def rows_of(pieces, row, rows):
    own, below, low, high, above = pieces
    mid = low.shape[0]
    apart = low[row : row + rows, :] if row < mid else high[row - mid : row - mid + rows, :]
    return [own[row : row + rows, :], below[row : row + rows, :], apart, above[row : row + rows, :]]


def forward_kernel(place, in_ref, own, below, low, high, above, tanh_ref, mine, other, part):
    pieces = (own, below, low, high, above)
    for o, first in enumerate(rows_of(pieces, 0, D)):
        tanh_ref[:, W * o : W * o + W] = jnp.tanh(dot(in_ref[...], first, ((1,), (0,))))
    for o in range(X):
        hidden = tanh_ref[:, W * o : W * o + W].astype(BF)
        for k in range(D // W):
            at = slice(W * k, W * k + W)
            more = dot(hidden, rows_of(pieces, D + W * k, W)[o], ((1,), (0,)))
            part[:, at] = more if o == 0 else part[:, at] + more
    half = mine.shape[1]

    @pl.when(place[1] == 0)
    def _():
        mine[...] = part[:, :half]
        other[...] = part[:, half:]

    @pl.when(place[1] != 0)
    def _():
        mine[...] = part[:, half:]
        other[...] = part[:, :half]


def back_kernel(place, inc_ref, own, below, low, high, above, out):
    half = out.shape[1]
    pieces = (own, below, low, high, above)
    for i in range(CORES):
        for o, piece in enumerate(rows_of(pieces, 2 * D + half * i, half)):
            at = W * (CORES * o + i)
            more = dot(inc_ref[:, at : at + W], piece, ((1,), (1,)))
            out[...] = more if i + o == 0 else out[...] + more


def put_sums(outs, o, in_ref, tanh_ref, all_ref, d1_ref, wt_ref, inc_ref, added=None):
    at = slice(W * o, W * o + W)
    g1 = dot(in_ref[...], d1_ref[:, at], ((0,), (0,)))
    g2 = dot(tanh_ref[:, at].astype(BF), all_ref[...], ((0,), (0,)))
    g3 = dot(wt_ref[...], inc_ref[:, 2 * W * o : 2 * W * o + 2 * W], ((0,), (0,)))
    share = Z // len(outs)

    def put(k, row, value):
        rows = value.shape[0]
        if added is not None and k in added[1]:
            value = value + added[0][k - added[1][0], row : row + rows, :].astype(F32)
        outs[k // share][k % share, row : row + rows, :] = value.astype(BF)

    for k in range(Z):
        put(k, 0, g1[W * k : W * k + W])
        put(k, 128, g2[:, W * k : W * k + W])
        put(k, 256, g3[64 * k : 64 * k + 64, :W])
        put(k, 320, g3[64 * k : 64 * k + 64, W:])


def far_kernel(
    place, in_ref, tanh_ref, own_ref, far_ref, own, below, w_low, w_high, above, wt_ref, inc_ref,
    error, low, high, all_ref, d1_ref, sent, back_ref
):
    sent[...] = error[...]
    half = own_ref.shape[1]

    @pl.when(place[1] == 0)
    def _():
        all_ref[:, :half] = own_ref[...]
        all_ref[:, half:] = far_ref[...]

    @pl.when(place[1] != 0)
    def _():
        all_ref[:, :half] = far_ref[...]
        all_ref[:, half:] = own_ref[...]

    pieces = (own, below, w_low, w_high, above)
    for o in range(X):
        at = slice(W * o, W * o + W)
        for k in range(D // W):
            d_second = all_ref[:, W * k : W * k + W]
            more = dot(d_second, rows_of(pieces, D + W * k, W)[o], ((1,), (1,)))
            back_ref[...] = more if k == 0 else back_ref[...] + more
        tanh = tanh_ref[:, at]
        d1_ref[:, at] = (back_ref[...] * (1.0 - tanh * tanh)).astype(BF)
    put_sums((low, high), 2, in_ref, tanh_ref, all_ref, d1_ref, wt_ref, inc_ref)


def own_kernel(place, in_ref, tanh_ref, all_ref, d1_ref, wt_ref, inc_ref, out, token):
    token[...] = jnp.zeros_like(token)
    put_sums((out,), 0, in_ref, tanh_ref, all_ref, d1_ref, wt_ref, inc_ref)


def near_kernel(
    place, in_ref, tanh_ref, all_ref, d1_ref, wt_ref, inc_ref, from_low, from_high, token, small, up, down
):
    rest = (in_ref, tanh_ref, all_ref, d1_ref, wt_ref, inc_ref)
    put_sums((up,), 3, *rest, (from_low, range(Z // 2)))
    put_sums((down,), 1, *rest, (from_high, range(Z // 2, Z)))


def sum_x_kernel(place, own, from_below, from_above, small_ref, *outs):
    rows = own.shape[1]
    small = two_words(small_ref[...])
    for r, out in enumerate(outs):
        k = lax.rem(place[3] + r, Z)
        out[:rows, :] = (
            own[k].astype(F32) + from_below[k].astype(F32) + from_above[k].astype(F32)
        ).astype(BF)
        out[rows:, :] = small


def sum_z_kernel(place, *refs):
    p, out, far = refs[:Z], refs[Z], refs[Z + 1]

    def total(row, rows):
        v = [ref[row : row + rows, :].astype(F32) for ref in p]
        return ((v[0] + v[4]) + (v[2] + v[6])) + ((v[1] + v[5]) + (v[3] + v[7]))

    for row in range(0, 320, 64):
        out[row : row + 64, :] = total(row, 64).astype(BF)
    far[...] = total(320, 64).astype(BF)
    words = total(384, 16)
    out[320:, :] = two_words(words[:8] + words[8:])


def pieces_kernel(place, main, far, out):
    out[:256, :] = main[:256, :]
    c = place[1]
    out[pl.ds(pl.multiple_of(256 + 64 * c, 64), 64), :] = main[256:320, :]
    out[pl.ds(pl.multiple_of(256 + 64 * (1 - c), 64), 64), :] = far[...]
    out[384:, :] = main[320:, :]


def out_kernel(place, own, below, above, low, high, first, second, third, loss, grad_y, grad_z):
    y = place[2]
    parts = [(own, 0, k, k) for k in range(Z)]
    parts += [(below, Y - 1, k, k) for k in range(Z)] + [(above, 1, k, k) for k in range(Z)]
    parts += [(low, 2, k, k) for k in range(Z // 2)]
    parts += [(high, 2, k, k + Z // 2) for k in range(Z // 2)]
    for ref, off, i, k in parts:
        at = lax.rem(y + off, Y)
        first[at, k] = ref[i, :128, :]
        second[at, :, W * k : W * k + W] = ref[i, 128:256, :]
        third[at, 0, k] = ref[i, 256:320, :]
        third[at, 1, k] = ref[i, 320:384, :]

    def words(ref):
        both = ref[0, 384:, :].astype(F32)
        return both[:8] + both[8:]

    small = (words(own) + words(low)) + (words(below) + words(above))
    grad_z[...] = small[0:1, :]
    loss[...] = small[1:2, 0:1]
    grad_y[...] = small[1:2, 1:2]


def factors_of(default_step, steps):
    counter = jnp.arange(steps, dtype=F32)
    factors = (
        1.0
        + DISCOUNT / steps
        - DEFAULT_LOSS * (counter[:, None] == default_step[None, :]).astype(F32)
    )
    coefs = [jnp.ones(default_step.shape, F32)]
    for n in range(steps - 1, 0, -1):
        coefs.append(coefs[-1] * factors[n])
    return factors, jnp.stack(coefs[::-1])


def local(
    x_start, y_start, z_start, increments, default_step, term_weight, w_first, w_second, w_third
):
    steps, paths, width = increments.shape
    tstep = 1.0 / steps
    scale = 1.0 / math.sqrt(paths * Y * Z)
    x, c, y, z = (lax.axis_index(name) for name in ("x", "core", "y", "z"))
    place = jnp.stack([x, c, y, z]).astype(jnp.int32)
    half = D // CORES
    flat = (2, paths // 2)

    third = w_third.reshape(X, CORES, half, width)
    far_third = core_swap(lax.dynamic_slice(third, (y, 1 - c, 0, 0), (1, 1, half, width))[0, 0])
    anywhere = pl.BlockSpec(memory_space=pl.ANY)
    packed = pl.pallas_call(
        pack_kernel,
        out_shape=jax.ShapeDtypeStruct((3 * D, width), BF),
        in_specs=[pl.BlockSpec(memory_space=pltpu.SMEM)] + [anywhere] * 4,
        out_specs=pl.BlockSpec(memory_space=pltpu.VMEM),
        scratch_shapes=[pltpu.SemaphoreType.DMA((3 + D // W,))],
        name="pack_kernel",
    )(place, w_first, w_second, third, far_third)
    increments, packed = lax.optimization_barrier((increments, packed))

    states = x_start[None, :] * (1.0 + DRIFT_RATE * tstep + VOLATILITY * increments[0])
    sends = []
    for n in range(1, steps):
        sends.append(jnp.stack([states.astype(BF), increments[n].astype(BF)]))
        states = states * (1.0 + DRIFT_RATE * tstep + VOLATILITY * increments[n])
    sends = jnp.stack(sends)
    rows = [pick(sends, y)] + [y_plus(pick(sends, (y + r) % Y), r) for r in range(1, Y)]
    rows = jnp.stack(rows)
    near = [pick(rows, (y - x + X) % X)]
    near += [x_plus(pick(rows, (y - x - q + 2 * X) % X), q) for q in range(1, X)]
    below, above = x_plus(packed, 1), x_plus(packed, 3)
    near, _, _ = lax.optimization_barrier((near, below, above))
    mid = 3 * D // 2
    low = x_plus(below[:mid], 1)
    high = x_plus(above[mid:], 3)
    weights = (packed, below, low, high, above)
    near = jnp.stack(near)
    far = core_swap(near)
    step_here = default_step.astype(F32)
    factors_here, coefs_here = factors_of(step_here, steps)
    target_part = jnp.sum(states * term_weight[None, :], axis=1) / math.sqrt(D)
    first_part = jnp.sum(increments[0] * z_start[None, :], axis=1)
    there = jnp.concatenate(
        [(coefs_here[0] * first_part - target_part).reshape(flat), step_here.reshape(flat)]
    )
    there = turned(there)
    part_sum = there[:2]
    factors, coefs = factors_of(there[2:].reshape(paths), steps)

    inputs, incs = vmem_call(
        arrange_kernel, place, (near, far), (((paths, D), BF), ((paths, D), BF))
    )
    tanh_first, mine, other = vmem_call(
        forward_kernel,
        place,
        (inputs, *weights),
        [((paths, half), F32)] * 3,
        [pltpu.VMEM((paths, D), F32)],
    )
    other = core_swap(other)
    (back,) = vmem_call(back_kernel, place, (incs, *weights), [((paths, half), F32)])
    tanh_second = jnp.tanh(mine + other)
    dots = jnp.sum(tanh_second * back, axis=1)
    coef = pick(coefs, y + 1)
    total = part_sum + (coef * dots).reshape(flat)
    total = total + core_swap(total)
    others = [y_plus(total, r) for r in range(1, Y)]
    total = (total + others[1]) + (others[0] + others[2])
    total = total + (factors[0] * coefs[0] * y_start).reshape(flat)
    adjoint = 2.0 * scale * total.reshape(paths)

    weight = (adjoint * coef)[:, None]
    weighted = (weight * tanh_second).astype(BF)
    d_second = (weight * back * (1.0 - tanh_second * tanh_second)).astype(BF)
    d_far = core_swap(d_second)
    low, high, d_all, d_first, sent = vmem_call(
        far_kernel,
        place,
        (inputs, tanh_first, d_second, d_far, *weights, weighted, incs, total),
        (
            ((Z // 2, 384, width), BF),
            ((Z // 2, 384, width), BF),
            ((paths, D), BF),
            ((paths, half), BF),
            (flat, F32),
        ),
        [pltpu.VMEM((paths, width), F32)],
    )
    error = turned(sent).reshape(paths)
    adjoint_one = 2.0 * scale * error * coefs_here[0]
    loss = scale * jnp.sum(error * error)
    grad_y = jnp.sum(adjoint_one * factors_here[0])
    grad_z = jnp.sum(adjoint_one[:, None] * increments[0], axis=0)
    small = jnp.concatenate(
        [grad_z, jnp.stack([loss, grad_y]), jnp.zeros((7 * width - 2,), F32)]
    ).reshape(8, width)

    low, high = x_plus(low, 1), x_plus(high, 3)
    shared = (inputs, tanh_first, d_all, d_first, weighted, incs)
    piece = ((Z, 384, width), BF)
    own, token = vmem_call(own_kernel, place, shared, (piece, ((8, width), F32)))
    up, down = vmem_call(
        near_kernel, place, (*shared, low, high, token, small), (piece, piece)
    )
    up, down = x_plus(up, 1), x_plus(down, 3)
    parts = vmem_call(
        sum_x_kernel, place, (own, up, down, small), [((400, width), BF)] * Z
    )
    parts = [parts[0]] + [z_plus(parts[r], r) for r in range(1, Z)]
    main, far = vmem_call(
        sum_z_kernel, place, parts, (((336, width), BF), ((64, width), BF))
    )
    (pieces,) = vmem_call(pieces_kernel, place, (main, core_swap(far)), (((400, width), BF),))
    own = lax.all_gather(pieces, "z")
    below, above = y_plus(own, 1), y_plus(own, 3)
    low, high = y_plus(below[: Z // 2], 1), y_plus(above[Z // 2 :], 3)
    first, second, third, loss, grad_y, grad_z = vmem_call(
        out_kernel,
        place,
        (own, below, above, low, high),
        (
            ((X, Z, 128, width), BF),
            ((X, 128, D), BF),
            ((X, CORES, Z, 64, width), BF),
            ((1, 1), F32),
            ((1, 1), F32),
            ((1, width), F32),
        ),
    )
    return (
        loss[0, 0],
        grad_y[0, 0],
        grad_z[0],
        first.reshape(X, D, width),
        second,
        third.reshape(X, D, width),
    )


def solution(mesh):
    axes = Mesh(mesh.devices.reshape(Z, Y, X, CORES), ("z", "y", "x", "core"))
    batch, dim = ("z", "y"), ("x", "core")
    placed = (
        P(dim),
        P(),
        P(dim),
        P(None, batch, dim),
        P(batch),
        P(dim),
        P(None, None, dim),
        P(None, dim, None),
        P(None, None, dim),
    )

    return jax.shard_map(
        local,
        mesh=axes,
        in_specs=placed,
        out_specs=(
            P(),
            P(),
            P(dim),
            P(None, None, dim),
            P(None, dim, None),
            P(None, None, dim),
        ),
        check_vma=False,
    )
```

profile of v0, /device:TPU:4, one launch (start us, length us, event | category | flops | bytes accessed | tf_op | source)
XLA Modules:
  0.0 218.5 jit_solution(8501902867147375208)
XLA Ops:
  3.7 2.7 %pack_kernel.1.own = bf16[3072,128]{1,0:T(8,128)(2,1)} custom-call(s32[4]{0:T(128)} %pad_add_fusion.place, bf16[4,1024,128]{2,1,0:T(8,128)(2,1)} %first.1, bf16[4,128,1024]{2,1,0:T(8,128)(2,1)} %second.1, bf16[4,2,512,128]{3,2,1,0:T(8,128)(2,1)} %bitcast.107, bf16[512,128]{1,0:T(8,128)(2,1)} %copy-done.19), custom_call_target="tpu_custom_call" | custom-call | tf_op jit(solution)/shard_map/pack_kernel/pallas_call | solution.py:290
  10.5 2.9 %collective-permute-start.2 = (bf16[2,256,128]{2,1,0:T(8,128)(2,1)S(1)}, bf16[2,256,128]{2,1,0:T(8,128)(2,1)S(1)}, u32[]{:S(2)}, u32[]{:S(2)}) collective-permute-start(bf16[2,256,128]{2,1,0:T(8,128)(2,1)S(1)} %get-tuple-element.105), channel_id=1, source_target_pairs={{0,16},{8,24},{16,0},{24,8},{1,17},{9,25},{17,1},{25,9},{2,18},{10... | collective-permute-start | bytes 393224 | tf_op jit(solution)/shard_map/ppermute | solution.py:26
  15.4 3.8 %collective-permute-done.2 = bf16[2,256,128]{2,1,0:T(8,128)(2,1)S(1)} collective-permute-done((bf16[2,256,128]{2,1,0:T(8,128)(2,1)S(1)}, bf16[2,256,128]{2,1,0:T(8,128)(2,1)S(1)}, u32[]{:S(2)}, u32[]{:S(2)}) %collective-permute-start.2) | collective-permute-done | bytes 131104 | tf_op jit(solution)/shard_map/ppermute | solution.py:26
  22.3 2.5 %collective-permute-start.6 = (bf16[2,256,128]{2,1,0:T(8,128)(2,1)S(1)}, bf16[2,256,128]{2,1,0:T(8,128)(2,1)S(1)}, u32[]{:S(2)}, u32[]{:S(2)}) collective-permute-start(bf16[2,256,128]{2,1,0:T(8,128)(2,1)S(1)} %get-tuple-element.99), channel_id=1, source_target_pairs={{0,6},{2,0},{4,2},{6,4},{1,7},{3,1},{5,3},{7,5},{8,14},{10,8},{12,... | collective-permute-start | bytes 393224 | tf_op jit(solution)/shard_map/ppermute | solution.py:26
  25.0 4.1 %collective-permute-done.4 = bf16[2,256,128]{2,1,0:T(8,128)(2,1)S(1)} collective-permute-done((bf16[2,256,128]{2,1,0:T(8,128)(2,1)S(1)}, bf16[2,256,128]{2,1,0:T(8,128)(2,1)S(1)}, u32[]{:S(2)}, u32[]{:S(2)}) %collective-permute-start.4) | collective-permute-done | bytes 131104 | tf_op jit(solution)/shard_map/ppermute | solution.py:26
  29.1 3.2 %collective-permute-done.5 = bf16[2,256,128]{2,1,0:T(8,128)(2,1)S(1)} collective-permute-done((bf16[2,256,128]{2,1,0:T(8,128)(2,1)S(1)}, bf16[2,256,128]{2,1,0:T(8,128)(2,1)S(1)}, u32[]{:S(2)}, u32[]{:S(2)}) %collective-permute-start.5) | collective-permute-done | bytes 131104 | tf_op jit(solution)/shard_map/ppermute | solution.py:26
  34.2 2.9 %collective-permute-start.10 = (bf16[1536,128]{1,0:T(8,128)(2,1)S(1)}, bf16[1536,128]{1,0:T(8,128)(2,1)S(1)}, u32[]{:S(2)}, u32[]{:S(2)}) collective-permute-start(bf16[1536,128]{1,0:T(8,128)(2,1)S(1)} %slice.90), channel_id=1, source_target_pairs={{0,2},{2,4},{4,6},{6,0},{1,3},{3,5},{5,7},{7,1},{8,10},{10,12},{12... | collective-permute-start | bytes 1179656 | tf_op jit(solution)/shard_map/ppermute | solution.py:26
  37.2 6.1 %collective-permute-start.12 = (f32[4,128]{1,0:T(4,128)S(1)}, f32[4,128]{1,0:T(4,128)S(1)}, u32[]{:S(2)}, u32[]{:S(2)}) collective-permute-start(f32[4,128]{1,0:T(4,128)S(1)} %pad_maximum_fusion.3), channel_id=1, source_target_pairs={{0,0},{2,8},{4,16},{6,24},{8,2},{10,10},{12,18},{14,26},{16,4},{18... | collective-permute-start | bytes 6152 | tf_op jit(solution)/shard_map/ppermute | solution.py:47
  44.0 3.5 %collective-permute-done.12 = f32[4,128]{1,0:T(4,128)S(1)} collective-permute-done((f32[4,128]{1,0:T(4,128)S(1)}, f32[4,128]{1,0:T(4,128)S(1)}, u32[]{:S(2)}, u32[]{:S(2)}) %collective-permute-start.12) | collective-permute-done | bytes 2080 | tf_op jit(solution)/shard_map/ppermute | solution.py:47
  47.6 2.5 %shard_map.136 = (bf16[256,1024]{1,0:T(8,128)(2,1)}, bf16[256,1024]{1,0:T(8,128)(2,1)}) custom-call(s32[4]{0:T(128)} %pad_add_fusion.place, bf16[4,2,256,128]{3,2,1,0:T(8,128)(2,1)} %copy-done.7, bf16[4,2,256,128]{3,2,1,0:T(8,128)(2,1)} %collective-permute-done.9.far), custom_call_target="tpu_custom_call" | custom-call | tf_op jit(solution)/shard_map/pallas_call | solution.py:64
  51.0 4.4 %shard_map.137 = (f32[256,512]{1,0:T(8,128)}, f32[256,512]{1,0:T(8,128)}, f32[256,512]{1,0:T(8,128)}) custom-call(s32[4]{0:T(128)} %pad_add_fusion.place, bf16[256,1024]{1,0:T(8,128)(2,1)} %get-tuple-element.48.in_ref, bf16[3072,128]{1,0:T(8,128)(2,1)} %pack_kernel.1.own, bf16[3072,128]{1,0:T(8,128)(2,1)} %copy-done, bf16[1536,128]{1,0:T(8,128)(2,1)} %copy-done.4, ...), custom_call_target="tpu_custom_call" | custom-call | tf_op jit(solution)/shard_map/pallas_call | solution.py:64
  55.6 3.6 %shard_map.138 = f32[256,512]{1,0:T(8,128)} custom-call(s32[4]{0:T(128)} %pad_add_fusion.place, bf16[256,1024]{1,0:T(8,128)(2,1)} %get-tuple-element.52.inc_ref, bf16[3072,128]{1,0:T(8,128)(2,1)} %pack_kernel.1.own, bf16[3072,128]{1,0:T(8,128)(2,1)} %copy-done, bf16[1536,128]{1,0:T(8,128)(2,1)} %copy-done.4, bf16[1536,128]{1,0:T(8,128)(2,1)} %copy-done.5, ...), custom_call_target="tpu_custom_call" | custom-call | tf_op jit(solution)/shard_map/pallas_call | solution.py:64
  61.8 2.7 %collective-permute-start.16 = (f32[2,128]{1,0:T(2,128)S(1)}, f32[2,128]{1,0:T(2,128)S(1)}, u32[]{:S(2)}, u32[]{:S(2)}) collective-permute-start(f32[2,128]{1,0:T(2,128)S(1)} %add.185), channel_id=1, source_target_pairs={{0,8},{8,16},{16,24},{24,0},{1,9},{9,17},{17,25},{25,1},{2,10},{10... | collective-permute-start | bytes 3080 | tf_op jit(solution)/shard_map/ppermute | solution.py:26
  71.7 4.7 %shard_map.139 = (bf16[4,384,128]{2,1,0:T(8,128)(2,1)}, bf16[4,384,128]{2,1,0:T(8,128)(2,1)}, bf16[256,1024]{1,0:T(8,128)(2,1)}, bf16[256,512]{1,0:T(8,128)(2,1)}, f32[2,128]{1,0:T(2,128)}) custom-call(s32[4]{0:T(128)} %pad_add_fusion.place, bf16[256,1024]{1,0:T(8,128)(2,1)} %get-tuple-element.48.in_ref, f32[256,512]{1,0:T(8,128)} %get-tuple-element.49.tanh_ref, ...), custom_call_target="tpu_custom_call" | custom-call | tf_op jit(solution)/shard_map/pallas_call | solution.py:64
  77.0 6.3 %collective-permute-start.21 = (f32[2,128]{1,0:T(2,128)S(1)}, f32[2,128]{1,0:T(2,128)S(1)}, u32[]{:S(2)}, u32[]{:S(2)}) collective-permute-start(f32[2,128]{1,0:T(2,128)S(1)} %copy-done.32), channel_id=1, source_target_pairs={{0,0},{2,8},{4,16},{6,24},{8,2},{10,10},{12,18},{14,26},{16,4},{18... | collective-permute-start | bytes 3080 | tf_op jit(solution)/shard_map/ppermute | solution.py:47
  83.3 3.0 %collective-permute-start.19 = (bf16[4,384,128]{2,1,0:T(8,128)(2,1)}, bf16[4,384,128]{2,1,0:T(8,128)(2,1)S(1)}, u32[]{:S(2)}, u32[]{:S(2)}) collective-permute-start(bf16[4,384,128]{2,1,0:T(8,128)(2,1)} %get-tuple-element.56), channel_id=1, source_target_pairs={{0,2},{2,4},{4,6},{6,0},{1,3},{3,5},{5,7},{7,1},{8,10},{10,12},{12... | collective-permute-start | bytes 1179656 | tf_op jit(solution)/shard_map/ppermute | solution.py:26
  86.3 3.1 %shard_map.140 = (bf16[8,384,128]{2,1,0:T(8,128)(2,1)}, f32[8,128]{1,0:T(8,128)}) custom-call(s32[4]{0:T(128)} %pad_add_fusion.place, bf16[256,1024]{1,0:T(8,128)(2,1)} %get-tuple-element.48.in_ref, f32[256,512]{1,0:T(8,128)} %get-tuple-element.49.tanh_ref, bf16[256,1024]{1,0:T(8,128)(2,1)} %get-tuple-element.53.all_ref, ...), custom_call_target="tpu_custom_call" | custom-call | tf_op jit(solution)/shard_map/pallas_call | solution.py:64
  97.9 3.6 %shard_map.141 = (bf16[8,384,128]{2,1,0:T(8,128)(2,1)}, bf16[8,384,128]{2,1,0:T(8,128)(2,1)}) custom-call(s32[4]{0:T(128)} %pad_add_fusion.place, bf16[256,1024]{1,0:T(8,128)(2,1)} %get-tuple-element.48.in_ref, f32[256,512]{1,0:T(8,128)} %get-tuple-element.49.tanh_ref, bf16[256,1024]{1,0:T(8,128)(2,1)} %get-tuple-element.53.all_ref, ...), custom_call_target="tpu_custom_call" | custom-call | tf_op jit(solution)/shard_map/pallas_call | solution.py:64
  103.5 16.3 %collective-permute-done.22.from_below = bf16[8,384,128]{2,1,0:T(8,128)(2,1)S(1)} collective-permute-done((bf16[8,384,128]{2,1,0:T(8,128)(2,1)}, bf16[8,384,128]{2,1,0:T(8,128)(2,1)S(1)}, u32[]{:S(2)}, u32[]{:S(2)}) %collective-permute-start.22) | collective-permute-done | bytes 786464 | tf_op jit(solution)/shard_map/ppermute | solution.py:26
  122.3 2.8 %shard_map.142 = (bf16[400,128]{1,0:T(8,128)(2,1)}, bf16[400,128]{1,0:T(8,128)(2,1)}, bf16[400,128]{1,0:T(8,128)(2,1)}, bf16[400,128]{1,0:T(8,128)(2,1)}, bf16[4...) custom-call(s32[4]{0:T(128)} %pad_add_fusion.place, ...), custom_call_target="tpu_custom_call" | custom-call | tf_op jit(solution)/shard_map/pallas_call | solution.py:64
  125.9 3.3 %collective-permute-start.25 = (bf16[400,128]{1,0:T(8,128)(2,1)}, bf16[400,128]{1,0:T(8,128)(2,1)S(1)}, u32[]{:S(2)}, u32[]{:S(2)}) collective-permute-start(bf16[400,128]{1,0:T(8,128)(2,1)} %get-tuple-element.64), channel_id=1, source_target_pairs={{0,64},{32,96},{64,128},{96,160},{128,192},{160,224},{192,0},{224,... | collective-permute-start | bytes 307208 | tf_op jit(solution)/shard_map/ppermute | solution.py:26
  129.1 4.0 %collective-permute-start.26 = (bf16[400,128]{1,0:T(8,128)(2,1)}, bf16[400,128]{1,0:T(8,128)(2,1)S(1)}, u32[]{:S(2)}, u32[]{:S(2)}) collective-permute-start(bf16[400,128]{1,0:T(8,128)(2,1)} %get-tuple-element.65), channel_id=1, source_target_pairs={{0,96},{32,128},{64,160},{96,192},{128,224},{160,0},{192,32},{224,... | collective-permute-start | bytes 307208 | tf_op jit(solution)/shard_map/ppermute | solution.py:26
  133.7 4.9 %collective-permute-start.28 = (bf16[400,128]{1,0:T(8,128)(2,1)}, bf16[400,128]{1,0:T(8,128)(2,1)S(1)}, u32[]{:S(2)}, u32[]{:S(2)}) collective-permute-start(bf16[400,128]{1,0:T(8,128)(2,1)} %get-tuple-element.67), channel_id=1, source_target_pairs={{0,160},{32,192},{64,224},{96,0},{128,32},{160,64},{192,96},{224,1... | collective-permute-start | bytes 307208 | tf_op jit(solution)/shard_map/ppermute | solution.py:26
  138.7 2.7 %collective-permute-start.29 = (bf16[400,128]{1,0:T(8,128)(2,1)}, bf16[400,128]{1,0:T(8,128)(2,1)S(1)}, u32[]{:S(2)}, u32[]{:S(2)}) collective-permute-start(bf16[400,128]{1,0:T(8,128)(2,1)} %get-tuple-element.68), channel_id=1, source_target_pairs={{0,192},{32,224},{64,0},{96,32},{128,64},{160,96},{192,128},{224,1... | collective-permute-start | bytes 307208 | tf_op jit(solution)/shard_map/ppermute | solution.py:26
  142.4 3.7 %collective-permute-done.26.refs_3_ = bf16[400,128]{1,0:T(8,128)(2,1)S(1)} collective-permute-done((bf16[400,128]{1,0:T(8,128)(2,1)}, bf16[400,128]{1,0:T(8,128)(2,1)S(1)}, u32[]{:S(2)}, u32[]{:S(2)}) %collective-permute-start.26) | collective-permute-done | bytes 102432 | tf_op jit(solution)/shard_map/ppermute | solution.py:26
  146.1 3.7 %collective-permute-done.28.refs_5_ = bf16[400,128]{1,0:T(8,128)(2,1)S(1)} collective-permute-done((bf16[400,128]{1,0:T(8,128)(2,1)}, bf16[400,128]{1,0:T(8,128)(2,1)S(1)}, u32[]{:S(2)}, u32[]{:S(2)}) %collective-permute-start.28) | collective-permute-done | bytes 102432 | tf_op jit(solution)/shard_map/ppermute | solution.py:26
  159.1 26.4 %all-gather = bf16[3200,128]{1,0:T(8,128)(2,1)S(1)} all-gather(bf16[400,128]{1,0:T(8,128)(2,1)} %shard_map.144), channel_id=2, replica_groups=mesh['z'=8,'y'=4,'x'=4,'core'=2] {'z'}, dimensions={0}, use_global_device_ids=true | all-gather | bytes 921600 | tf_op jit(solution)/shard_map/all_gather | solution.py:393
  185.5 3.2 %collective-permute-start.33 = (bf16[8,400,128]{2,1,0:T(8,128)(2,1)S(1)}, bf16[8,400,128]{2,1,0:T(8,128)(2,1)S(1)}, u32[]{:S(2)}, u32[]{:S(2)}) collective-permute-start(bf16[8,400,128]{2,1,0:T(8,128)(2,1)S(1)} %bitcast.104), channel_id=1, source_target_pairs={{0,24},{8,0},{16,8},{24,16},{1,25},{9,1},{17,9},{25,17},{2,26},{10... | collective-permute-start | bytes 2457608 | tf_op jit(solution)/shard_map/ppermute | solution.py:26
  188.8 15.1 %collective-permute-done.32.below = bf16[8,400,128]{2,1,0:T(8,128)(2,1)S(1)} collective-permute-done((bf16[8,400,128]{2,1,0:T(8,128)(2,1)S(1)}, bf16[8,400,128]{2,1,0:T(8,128)(2,1)S(1)}, u32[]{:S(2)}, u32[]{:S(2)}) %collective-permute-start.32) | collective-permute-done | bytes 819232 | tf_op jit(solution)/shard_map/ppermute | solution.py:26
  204.0 3.3 %collective-permute-start.35 = (bf16[4,400,128]{2,1,0:T(8,128)(2,1)S(1)}, bf16[4,400,128]{2,1,0:T(8,128)(2,1)S(1)}, u32[]{:S(2)}, u32[]{:S(2)}) collective-permute-start(bf16[4,400,128]{2,1,0:T(8,128)(2,1)S(1)} %slice.103), channel_id=1, source_target_pairs={{0,24},{8,0},{16,8},{24,16},{1,25},{9,1},{17,9},{25,17},{2,26},{10... | collective-permute-start | bytes 1228808 | tf_op jit(solution)/shard_map/ppermute | solution.py:26
  207.3 5.8 %collective-permute-done.34.low = bf16[4,400,128]{2,1,0:T(8,128)(2,1)S(1)} collective-permute-done((bf16[4,400,128]{2,1,0:T(8,128)(2,1)S(1)}, bf16[4,400,128]{2,1,0:T(8,128)(2,1)S(1)}, u32[]{:S(2)}, u32[]{:S(2)}) %collective-permute-start.34) | collective-permute-done | bytes 409632 | tf_op jit(solution)/shard_map/ppermute | solution.py:26
  214.6 3.9 %shard_map.145 = (bf16[4,8,128,128]{3,2,1,0:T(8,128)(2,1)}, bf16[4,128,1024]{2,1,0:T(8,128)(2,1)}, bf16[4,2,8,64,128]{4,3,2,1,0:T(8,128)(2,1)}, f32[1,1]{1,0:T(1...) custom-call(s32[4]{0:T(128)} %pad_add_fusion.place, bf16[8,400,128]{2,1,0:T(8,128)(2,1)} %bitcast.105, ...), custom_call_target="tpu_custom_call" | custom-call | tf_op jit(solution)/shard_map/pallas_call | solution.py:64
  (156 shorter events, 51.2 us)
Async XLA Ops:
  6.4 26.9 %collective-permute-start.7 = (bf16[3072,128]{1,0:T(8,128)(2,1)}, bf16[3072,128]{1,0:T(8,128)(2,1)S(1)}, u32[]{:S(2)}, u32[]{:S(2)}) collective-permute-start(bf16[3072,128]{1,0:T(8,128)(2,1)} %pack_kernel.1.own), channel_id=1, source_target_pairs={{0,2},{2,4},{4,6},{6,0},{1,3},{3,5},{5,7},{7,1},{8,10},{10,12},{12... | collective-permute-start | bytes 2359304 | tf_op jit(solution)/shard_map/ppermute | solution.py:26
  7.7 25.7 %collective-permute-start.8 = (bf16[3072,128]{1,0:T(8,128)(2,1)}, bf16[3072,128]{1,0:T(8,128)(2,1)S(1)}, u32[]{:S(2)}, u32[]{:S(2)}) collective-permute-start(bf16[3072,128]{1,0:T(8,128)(2,1)} %pack_kernel.1.own), channel_id=1, source_target_pairs={{0,6},{2,0},{4,2},{6,4},{1,7},{3,1},{5,3},{7,5},{8,14},{10,8},{12,... | collective-permute-start | bytes 2359304 | tf_op jit(solution)/shard_map/ppermute | solution.py:26
  8.9 6.5 %collective-permute-start.1 = (bf16[2,256,128]{2,1,0:T(8,128)(2,1)S(1)}, bf16[2,256,128]{2,1,0:T(8,128)(2,1)S(1)}, u32[]{:S(2)}, u32[]{:S(2)}) collective-permute-start(bf16[2,256,128]{2,1,0:T(8,128)(2,1)S(1)} %get-tuple-element.106), channel_id=1, source_target_pairs={{0,8},{8,16},{16,24},{24,0},{1,9},{9,17},{17,25},{25,1},{2,10},{10... | collective-permute-start | bytes 393224 | tf_op jit(solution)/shard_map/ppermute | solution.py:26
  10.5 8.7 %collective-permute-start.2 = (bf16[2,256,128]{2,1,0:T(8,128)(2,1)S(1)}, bf16[2,256,128]{2,1,0:T(8,128)(2,1)S(1)}, u32[]{:S(2)}, u32[]{:S(2)}) collective-permute-start(bf16[2,256,128]{2,1,0:T(8,128)(2,1)S(1)} %get-tuple-element.105), channel_id=1, source_target_pairs={{0,16},{8,24},{16,0},{24,8},{1,17},{9,25},{17,1},{25,9},{2,18},{10... | collective-permute-start | bytes 393224 | tf_op jit(solution)/shard_map/ppermute | solution.py:26
  13.4 5.8 %collective-permute-start.3 = (bf16[2,256,128]{2,1,0:T(8,128)(2,1)S(1)}, bf16[2,256,128]{2,1,0:T(8,128)(2,1)S(1)}, u32[]{:S(2)}, u32[]{:S(2)}) collective-permute-start(bf16[2,256,128]{2,1,0:T(8,128)(2,1)S(1)} %get-tuple-element.104), channel_id=1, source_target_pairs={{0,24},{8,0},{16,8},{24,16},{1,25},{9,1},{17,9},{25,17},{2,26},{10... | collective-permute-start | bytes 393224 | tf_op jit(solution)/shard_map/ppermute | solution.py:26
  19.3 9.8 %collective-permute-start.4 = (bf16[2,256,128]{2,1,0:T(8,128)(2,1)S(1)}, bf16[2,256,128]{2,1,0:T(8,128)(2,1)S(1)}, u32[]{:S(2)}, u32[]{:S(2)}) collective-permute-start(bf16[2,256,128]{2,1,0:T(8,128)(2,1)S(1)} %get-tuple-element.101), channel_id=1, source_target_pairs={{0,2},{2,4},{4,6},{6,0},{1,3},{3,5},{5,7},{7,1},{8,10},{10,12},{12... | collective-permute-start | bytes 393224 | tf_op jit(solution)/shard_map/ppermute | solution.py:26
  20.6 11.8 %collective-permute-start.5 = (bf16[2,256,128]{2,1,0:T(8,128)(2,1)S(1)}, bf16[2,256,128]{2,1,0:T(8,128)(2,1)S(1)}, u32[]{:S(2)}, u32[]{:S(2)}) collective-permute-start(bf16[2,256,128]{2,1,0:T(8,128)(2,1)S(1)} %get-tuple-element.100), channel_id=1, source_target_pairs={{0,4},{2,6},{4,0},{6,2},{1,5},{3,7},{5,1},{7,3},{8,12},{10,14},{12... | collective-permute-start | bytes 393224 | tf_op jit(solution)/shard_map/ppermute | solution.py:26
  22.3 11.0 %collective-permute-start.6 = (bf16[2,256,128]{2,1,0:T(8,128)(2,1)S(1)}, bf16[2,256,128]{2,1,0:T(8,128)(2,1)S(1)}, u32[]{:S(2)}, u32[]{:S(2)}) collective-permute-start(bf16[2,256,128]{2,1,0:T(8,128)(2,1)S(1)} %get-tuple-element.99), channel_id=1, source_target_pairs={{0,6},{2,0},{4,2},{6,4},{1,7},{3,1},{5,3},{7,5},{8,14},{10,8},{12,... | collective-permute-start | bytes 393224 | tf_op jit(solution)/shard_map/ppermute | solution.py:26
  33.4 14.2 %collective-permute-start.9 = (bf16[4,2,256,128]{3,2,1,0:T(8,128)(2,1)S(1)}, bf16[4,2,256,128]{3,2,1,0:T(8,128)(2,1)}, u32[]{:S(2)}, u32[]{:S(2)}) collective-permute-start(bf16[4,2,256,128]{3,2,1,0:T(8,128)(2,1)S(1)} %pad_maximum_fusion.2.near), channel_id=1, source_target_pairs={{0,1},{1,0},{2,3},{3,2},{4,5},{5,4},{6,7},{7,6},{8,9},{9,8},{10,11... | collective-permute-start | bytes 1572872 | tf_op jit(solution)/shard_map/ppermute | solution.py:30
  34.2 15.9 %collective-permute-start.10 = (bf16[1536,128]{1,0:T(8,128)(2,1)S(1)}, bf16[1536,128]{1,0:T(8,128)(2,1)S(1)}, u32[]{:S(2)}, u32[]{:S(2)}) collective-permute-start(bf16[1536,128]{1,0:T(8,128)(2,1)S(1)} %slice.90), channel_id=1, source_target_pairs={{0,2},{2,4},{4,6},{6,0},{1,3},{3,5},{5,7},{7,1},{8,10},{10,12},{12... | collective-permute-start | bytes 1179656 | tf_op jit(solution)/shard_map/ppermute | solution.py:26
  37.1 13.0 %collective-permute-start.11 = (bf16[1536,128]{1,0:T(8,128)(2,1)S(1)}, bf16[1536,128]{1,0:T(8,128)(2,1)S(1)}, u32[]{:S(2)}, u32[]{:S(2)}) collective-permute-start(bf16[1536,128]{1,0:T(8,128)(2,1)S(1)} %slice.91), channel_id=1, source_target_pairs={{0,6},{2,0},{4,2},{6,4},{1,7},{3,1},{5,3},{7,5},{8,14},{10,8},{12,... | collective-permute-start | bytes 1179656 | tf_op jit(solution)/shard_map/ppermute | solution.py:26
  37.2 10.3 %collective-permute-start.12 = (f32[4,128]{1,0:T(4,128)S(1)}, f32[4,128]{1,0:T(4,128)S(1)}, u32[]{:S(2)}, u32[]{:S(2)}) collective-permute-start(f32[4,128]{1,0:T(4,128)S(1)} %pad_maximum_fusion.3), channel_id=1, source_target_pairs={{0,0},{2,8},{4,16},{6,24},{8,2},{10,10},{12,18},{14,26},{16,4},{18... | collective-permute-start | bytes 6152 | tf_op jit(solution)/shard_map/ppermute | solution.py:47
  55.5 3.7 %collective-permute-start.13 = (f32[256,512]{1,0:T(8,128)}, f32[256,512]{1,0:T(8,128)S(1)}, u32[]{:S(2)}, u32[]{:S(2)}) collective-permute-start(f32[256,512]{1,0:T(8,128)} %get-tuple-element.51), channel_id=1, source_target_pairs={{0,1},{1,0},{2,3},{3,2},{4,5},{5,4},{6,7},{7,6},{8,9},{9,8},{10,11... | collective-permute-start | bytes 1572872 | tf_op jit(solution)/shard_map/ppermute | solution.py:30
  61.8 5.1 %collective-permute-start.15 = (f32[2,128]{1,0:T(2,128)S(1)}, f32[2,128]{1,0:T(2,128)S(1)}, u32[]{:S(2)}, u32[]{:S(2)}) collective-permute-start(f32[2,128]{1,0:T(2,128)S(1)} %add.185), channel_id=1, source_target_pairs={{0,16},{8,24},{16,0},{24,8},{1,17},{9,25},{17,1},{25,9},{2,18},{10... | collective-permute-start | bytes 3080 | tf_op jit(solution)/shard_map/ppermute | solution.py:26
  61.8 5.1 %collective-permute-start.16 = (f32[2,128]{1,0:T(2,128)S(1)}, f32[2,128]{1,0:T(2,128)S(1)}, u32[]{:S(2)}, u32[]{:S(2)}) collective-permute-start(f32[2,128]{1,0:T(2,128)S(1)} %add.185), channel_id=1, source_target_pairs={{0,8},{8,16},{16,24},{24,0},{1,9},{9,17},{17,25},{25,1},{2,10},{10... | collective-permute-start | bytes 3080 | tf_op jit(solution)/shard_map/ppermute | solution.py:26
  64.5 3.6 %collective-permute-start.17 = (f32[2,128]{1,0:T(2,128)S(1)}, f32[2,128]{1,0:T(2,128)S(1)}, u32[]{:S(2)}, u32[]{:S(2)}) collective-permute-start(f32[2,128]{1,0:T(2,128)S(1)} %add.185), channel_id=1, source_target_pairs={{0,24},{8,0},{16,8},{24,16},{1,25},{9,1},{17,9},{25,17},{2,26},{10... | collective-permute-start | bytes 3080 | tf_op jit(solution)/shard_map/ppermute | solution.py:26
  77.0 12.4 %collective-permute-start.21 = (f32[2,128]{1,0:T(2,128)S(1)}, f32[2,128]{1,0:T(2,128)S(1)}, u32[]{:S(2)}, u32[]{:S(2)}) collective-permute-start(f32[2,128]{1,0:T(2,128)S(1)} %copy-done.32), channel_id=1, source_target_pairs={{0,0},{2,8},{4,16},{6,24},{8,2},{10,10},{12,18},{14,26},{16,4},{18... | collective-permute-start | bytes 3080 | tf_op jit(solution)/shard_map/ppermute | solution.py:47
  83.3 11.7 %collective-permute-start.19 = (bf16[4,384,128]{2,1,0:T(8,128)(2,1)}, bf16[4,384,128]{2,1,0:T(8,128)(2,1)S(1)}, u32[]{:S(2)}, u32[]{:S(2)}) collective-permute-start(bf16[4,384,128]{2,1,0:T(8,128)(2,1)} %get-tuple-element.56), channel_id=1, source_target_pairs={{0,2},{2,4},{4,6},{6,0},{1,3},{3,5},{5,7},{7,1},{8,10},{10,12},{12... | collective-permute-start | bytes 1179656 | tf_op jit(solution)/shard_map/ppermute | solution.py:26
  86.3 10.8 %collective-permute-start.20 = (bf16[4,384,128]{2,1,0:T(8,128)(2,1)}, bf16[4,384,128]{2,1,0:T(8,128)(2,1)S(1)}, u32[]{:S(2)}, u32[]{:S(2)}) collective-permute-start(bf16[4,384,128]{2,1,0:T(8,128)(2,1)} %get-tuple-element.57), channel_id=1, source_target_pairs={{0,6},{2,0},{4,2},{6,4},{1,7},{3,1},{5,3},{7,5},{8,14},{10,8},{12,... | collective-permute-start | bytes 1179656 | tf_op jit(solution)/shard_map/ppermute | solution.py:26
  101.5 18.4 %collective-permute-start.22 = (bf16[8,384,128]{2,1,0:T(8,128)(2,1)}, bf16[8,384,128]{2,1,0:T(8,128)(2,1)S(1)}, u32[]{:S(2)}, u32[]{:S(2)}) collective-permute-start(bf16[8,384,128]{2,1,0:T(8,128)(2,1)} %get-tuple-element.60), channel_id=1, source_target_pairs={{0,2},{2,4},{4,6},{6,0},{1,3},{3,5},{5,7},{7,1},{8,10},{10,12},{12... | collective-permute-start | bytes 2359304 | tf_op jit(solution)/shard_map/ppermute | solution.py:26
  103.0 18.4 %collective-permute-start.23 = (bf16[8,384,128]{2,1,0:T(8,128)(2,1)}, bf16[8,384,128]{2,1,0:T(8,128)(2,1)S(1)}, u32[]{:S(2)}, u32[]{:S(2)}) collective-permute-start(bf16[8,384,128]{2,1,0:T(8,128)(2,1)} %get-tuple-element.61), channel_id=1, source_target_pairs={{0,6},{2,0},{4,2},{6,4},{1,7},{3,1},{5,3},{7,5},{8,14},{10,8},{12,... | collective-permute-start | bytes 2359304 | tf_op jit(solution)/shard_map/ppermute | solution.py:26
  125.1 13.6 %collective-permute-start.24 = (bf16[400,128]{1,0:T(8,128)(2,1)}, bf16[400,128]{1,0:T(8,128)(2,1)S(1)}, u32[]{:S(2)}, u32[]{:S(2)}) collective-permute-start(bf16[400,128]{1,0:T(8,128)(2,1)} %get-tuple-element.63), channel_id=1, source_target_pairs={{0,32},{32,64},{64,96},{96,128},{128,160},{160,192},{192,224},{224... | collective-permute-start | bytes 307208 | tf_op jit(solution)/shard_map/ppermute | solution.py:26
  125.9 16.5 %collective-permute-start.25 = (bf16[400,128]{1,0:T(8,128)(2,1)}, bf16[400,128]{1,0:T(8,128)(2,1)S(1)}, u32[]{:S(2)}, u32[]{:S(2)}) collective-permute-start(bf16[400,128]{1,0:T(8,128)(2,1)} %get-tuple-element.64), channel_id=1, source_target_pairs={{0,64},{32,96},{64,128},{96,160},{128,192},{160,224},{192,0},{224,... | collective-permute-start | bytes 307208 | tf_op jit(solution)/shard_map/ppermute | solution.py:26
  129.1 16.9 %collective-permute-start.26 = (bf16[400,128]{1,0:T(8,128)(2,1)}, bf16[400,128]{1,0:T(8,128)(2,1)S(1)}, u32[]{:S(2)}, u32[]{:S(2)}) collective-permute-start(bf16[400,128]{1,0:T(8,128)(2,1)} %get-tuple-element.65), channel_id=1, source_target_pairs={{0,96},{32,128},{64,160},{96,192},{128,224},{160,0},{192,32},{224,... | collective-permute-start | bytes 307208 | tf_op jit(solution)/shard_map/ppermute | solution.py:26
  133.2 12.9 %collective-permute-start.27 = (bf16[400,128]{1,0:T(8,128)(2,1)}, bf16[400,128]{1,0:T(8,128)(2,1)S(1)}, u32[]{:S(2)}, u32[]{:S(2)}) collective-permute-start(bf16[400,128]{1,0:T(8,128)(2,1)} %get-tuple-element.66), channel_id=1, source_target_pairs={{0,128},{32,160},{64,192},{96,224},{128,0},{160,32},{192,64},{224,... | collective-permute-start | bytes 307208 | tf_op jit(solution)/shard_map/ppermute | solution.py:26
  133.7 16.0 %collective-permute-start.28 = (bf16[400,128]{1,0:T(8,128)(2,1)}, bf16[400,128]{1,0:T(8,128)(2,1)S(1)}, u32[]{:S(2)}, u32[]{:S(2)}) collective-permute-start(bf16[400,128]{1,0:T(8,128)(2,1)} %get-tuple-element.67), channel_id=1, source_target_pairs={{0,160},{32,192},{64,224},{96,0},{128,32},{160,64},{192,96},{224,1... | collective-permute-start | bytes 307208 | tf_op jit(solution)/shard_map/ppermute | solution.py:26
  138.7 12.7 %collective-permute-start.29 = (bf16[400,128]{1,0:T(8,128)(2,1)}, bf16[400,128]{1,0:T(8,128)(2,1)S(1)}, u32[]{:S(2)}, u32[]{:S(2)}) collective-permute-start(bf16[400,128]{1,0:T(8,128)(2,1)} %get-tuple-element.68), channel_id=1, source_target_pairs={{0,192},{32,224},{64,0},{96,32},{128,64},{160,96},{192,128},{224,1... | collective-permute-start | bytes 307208 | tf_op jit(solution)/shard_map/ppermute | solution.py:26
  142.4 10.6 %collective-permute-start.30 = (bf16[400,128]{1,0:T(8,128)(2,1)}, bf16[400,128]{1,0:T(8,128)(2,1)S(1)}, u32[]{:S(2)}, u32[]{:S(2)}) collective-permute-start(bf16[400,128]{1,0:T(8,128)(2,1)} %get-tuple-element.69), channel_id=1, source_target_pairs={{0,224},{32,0},{64,32},{96,64},{128,96},{160,128},{192,160},{224,1... | collective-permute-start | bytes 307208 | tf_op jit(solution)/shard_map/ppermute | solution.py:26
  185.5 18.3 %collective-permute-start.32 = (bf16[8,400,128]{2,1,0:T(8,128)(2,1)S(1)}, bf16[8,400,128]{2,1,0:T(8,128)(2,1)S(1)}, u32[]{:S(2)}, u32[]{:S(2)}) collective-permute-start(bf16[8,400,128]{2,1,0:T(8,128)(2,1)S(1)} %bitcast.103), channel_id=1, source_target_pairs={{0,8},{8,16},{16,24},{24,0},{1,9},{9,17},{17,25},{25,1},{2,10},{10... | collective-permute-start | bytes 2457608 | tf_op jit(solution)/shard_map/ppermute | solution.py:26
  185.5 18.4 %collective-permute-start.33 = (bf16[8,400,128]{2,1,0:T(8,128)(2,1)S(1)}, bf16[8,400,128]{2,1,0:T(8,128)(2,1)S(1)}, u32[]{:S(2)}, u32[]{:S(2)}) collective-permute-start(bf16[8,400,128]{2,1,0:T(8,128)(2,1)S(1)} %bitcast.104), channel_id=1, source_target_pairs={{0,24},{8,0},{16,8},{24,16},{1,25},{9,1},{17,9},{25,17},{2,26},{10... | collective-permute-start | bytes 2457608 | tf_op jit(solution)/shard_map/ppermute | solution.py:26
  203.9 9.2 %collective-permute-start.34 = (bf16[4,400,128]{2,1,0:T(8,128)(2,1)S(1)}, bf16[4,400,128]{2,1,0:T(8,128)(2,1)S(1)}, u32[]{:S(2)}, u32[]{:S(2)}) collective-permute-start(bf16[4,400,128]{2,1,0:T(8,128)(2,1)S(1)} %slice.102), channel_id=1, source_target_pairs={{0,8},{8,16},{16,24},{24,0},{1,9},{9,17},{17,25},{25,1},{2,10},{10... | collective-permute-start | bytes 1228808 | tf_op jit(solution)/shard_map/ppermute | solution.py:26
  204.0 9.1 %collective-permute-start.35 = (bf16[4,400,128]{2,1,0:T(8,128)(2,1)S(1)}, bf16[4,400,128]{2,1,0:T(8,128)(2,1)S(1)}, u32[]{:S(2)}, u32[]{:S(2)}) collective-permute-start(bf16[4,400,128]{2,1,0:T(8,128)(2,1)S(1)} %slice.103), channel_id=1, source_target_pairs={{0,24},{8,0},{16,8},{24,16},{1,25},{9,1},{17,9},{25,17},{2,26},{10... | collective-permute-start | bytes 1228808 | tf_op jit(solution)/shard_map/ppermute | solution.py:26
  (37 other events, 138.3 us)
where the time goes:
time: 220 us; the launch traced here: 219 us
  waiting for transfers between devices  78.4 us (36%)
  starting transfers between devices  60.8 us (28%)
  Pallas kernels  34.8 us (16%)
  blocking collectives  26.4 us (12%)
  local copies, waits for them, and re-layouts  9.06 us (4%)
  other arithmetic  6.59 us (3%)
  between operations  2.46 us (1%)
    ppermute x28, waiting for transfers between devices, shifted(): return lax.ppermute(value, axis, [(i, (i + o) % n) for i in range(n)])  70.6 us
    ppermute x28, starting transfers between devices, shifted(): return lax.ppermute(value, axis, [(i, (i + o) % n) for i in range(n)])  47.6 us
    pallas_call x10, Pallas kernels, vmem_call(): pl.pallas_call(kernel, out_shape=[jax.ShapeDtypeStruct(shape, dtype) for...  32.1 us
    all_gather x1, blocking collectives, local(): own = lax.all_gather(pieces, 'z')  26.4 us
    ppermute x2, starting transfers between devices, turned(): return lax.ppermute(value, ('y', 'x'), pairs)  12.4 us
    unnamed x66, local copies, waits for them, and re-layouts  7.86 us
  transfers between devices with their start and end apart: 36, of which 23 were waited for; matrix products, arithmetic and copies ran while one was open for 2% of the time, Pallas kernels for 4%

commit v1 on v0

--- a/solution.py
+++ b/solution.py
@@ -18,6 +18,7 @@
 
 X, CORES, Y, Z = 4, 2, 4, 8
 W = D // (X * CORES)
+ROOM = 20 << 20
 BF = jnp.bfloat16
 F32 = jnp.float32
 
@@ -67,6 +68,7 @@
         in_specs=[pl.BlockSpec(memory_space=pltpu.SMEM)] + [vmem] * len(args),
         out_specs=[vmem] * len(outs),
         scratch_shapes=list(scratch),
+        compiler_params=pltpu.CompilerParams(vmem_limit_bytes=ROOM),
     )(place, *args)
 
 
@@ -91,13 +93,13 @@
     copies = [
         (first.at[y], out.at[:D, :]),
         (third.at[y, c], out.at[2 * D : 2 * D + half, :]),
-        (far, out.at[2 * D + half :, :]),
     ]
     for k in range(D // W):
         copies.append((second.at[y, :, pl.ds(W * k, W)], out.at[D + W * k : D + W * k + W, :]))
     copies = [pltpu.make_async_copy(a, b, sems.at[i]) for i, (a, b) in enumerate(copies)]
     for copy in copies:
         copy.start()
+    out[2 * D + half :, :] = far[...]
     for copy in copies:
         copy.wait()
 
@@ -189,6 +191,28 @@
         tanh = tanh_ref[:, at]
         d1_ref[:, at] = (back_ref[...] * (1.0 - tanh * tanh)).astype(BF)
     put_sums((low, high), 2, in_ref, tanh_ref, all_ref, d1_ref, wt_ref, inc_ref)
+
+
+def small_kernel(place, error, coef, factor, inc_ref, out):
+    scale = 1.0 / math.sqrt(inc_ref.shape[0] * Y * Z)
+    err = error[...]
+    adjoint = 2.0 * scale * err * coef[...]
+    rows = inc_ref.shape[0] // 2
+    for i in range(2):
+        more = lax.dot_general(
+            jnp.broadcast_to(adjoint[i : i + 1, :], (8, rows)),
+            inc_ref[rows * i : rows * (i + 1), :],
+            (((1,), (0,)), ((), ())),
+            precision=lax.Precision.HIGHEST,
+            preferred_element_type=F32,
+        )
+        grad_z = more if i == 0 else grad_z + more
+    loss = scale * jnp.sum(err * err)
+    grad_y = jnp.sum(adjoint * factor[...])
+    row = lax.broadcasted_iota(jnp.int32, (8, W), 0)
+    lane = lax.broadcasted_iota(jnp.int32, (8, W), 1)
+    scalars = jnp.where(lane == 0, loss, jnp.where(lane == 1, grad_y, 0.0))
+    out[...] = jnp.where(row == 0, grad_z, jnp.where(row == 1, scalars, 0.0))
 
 
 def own_kernel(place, in_ref, tanh_ref, all_ref, d1_ref, wt_ref, inc_ref, out, token):
@@ -286,13 +310,13 @@
 
     third = w_third.reshape(X, CORES, half, width)
     far_third = core_swap(lax.dynamic_slice(third, (y, 1 - c, 0, 0), (1, 1, half, width))[0, 0])
-    anywhere = pl.BlockSpec(memory_space=pl.ANY)
+    hbm, vmem = (pl.BlockSpec(memory_space=space) for space in (pltpu.HBM, pltpu.VMEM))
     packed = pl.pallas_call(
         pack_kernel,
         out_shape=jax.ShapeDtypeStruct((3 * D, width), BF),
-        in_specs=[pl.BlockSpec(memory_space=pltpu.SMEM)] + [anywhere] * 4,
-        out_specs=pl.BlockSpec(memory_space=pltpu.VMEM),
-        scratch_shapes=[pltpu.SemaphoreType.DMA((3 + D // W,))],
+        in_specs=[pl.BlockSpec(memory_space=pltpu.SMEM), hbm, hbm, hbm, vmem],
+        out_specs=vmem,
+        scratch_shapes=[pltpu.SemaphoreType.DMA((2 + D // W,))],
         name="pack_kernel",
     )(place, w_first, w_second, third, far_third)
     increments, packed = lax.optimization_barrier((increments, packed))
@@ -304,27 +328,25 @@
         states = states * (1.0 + DRIFT_RATE * tstep + VOLATILITY * increments[n])
     sends = jnp.stack(sends)
     rows = [pick(sends, y)] + [y_plus(pick(sends, (y + r) % Y), r) for r in range(1, Y)]
+    step_here = default_step.astype(F32)
+    factors_here, coefs_here = factors_of(step_here, steps)
+    target_part = jnp.sum(states * term_weight[None, :], axis=1) / math.sqrt(D)
+    first_part = jnp.sum(increments[0] * z_start[None, :], axis=1)
+    there = jnp.concatenate(
+        [(coefs_here[0] * first_part - target_part).reshape(flat), step_here.reshape(flat)]
+    )
+    rows, there = lax.optimization_barrier((rows, there))
     rows = jnp.stack(rows)
     near = [pick(rows, (y - x + X) % X)]
     near += [x_plus(pick(rows, (y - x - q + 2 * X) % X), q) for q in range(1, X)]
     below, above = x_plus(packed, 1), x_plus(packed, 3)
-    near, _, _ = lax.optimization_barrier((near, below, above))
     mid = 3 * D // 2
     low = x_plus(below[:mid], 1)
     high = x_plus(above[mid:], 3)
     weights = (packed, below, low, high, above)
     near = jnp.stack(near)
     far = core_swap(near)
-    step_here = default_step.astype(F32)
-    factors_here, coefs_here = factors_of(step_here, steps)
-    target_part = jnp.sum(states * term_weight[None, :], axis=1) / math.sqrt(D)
-    first_part = jnp.sum(increments[0] * z_start[None, :], axis=1)
-    there = jnp.concatenate(
-        [(coefs_here[0] * first_part - target_part).reshape(flat), step_here.reshape(flat)]
-    )
     there = turned(there)
-    part_sum = there[:2]
-    factors, coefs = factors_of(there[2:].reshape(paths), steps)
 
     inputs, incs = vmem_call(
         arrange_kernel, place, (near, far), (((paths, D), BF), ((paths, D), BF))
@@ -336,6 +358,9 @@
         [((paths, half), F32)] * 3,
         [pltpu.VMEM((paths, D), F32)],
     )
+    there, _ = lax.optimization_barrier((there, mine))
+    part_sum = there[:2]
+    factors, coefs = factors_of(there[2:].reshape(paths), steps)
     other = core_swap(other)
     (back,) = vmem_call(back_kernel, place, (incs, *weights), [((paths, half), F32)])
     tanh_second = jnp.tanh(mine + other)
@@ -365,15 +390,12 @@
         ),
         [pltpu.VMEM((paths, width), F32)],
     )
-    error = turned(sent).reshape(paths)
-    adjoint_one = 2.0 * scale * error * coefs_here[0]
-    loss = scale * jnp.sum(error * error)
-    grad_y = jnp.sum(adjoint_one * factors_here[0])
-    grad_z = jnp.sum(adjoint_one[:, None] * increments[0], axis=0)
-    small = jnp.concatenate(
-        [grad_z, jnp.stack([loss, grad_y]), jnp.zeros((7 * width - 2,), F32)]
-    ).reshape(8, width)
-
+    (small,) = vmem_call(
+        small_kernel,
+        place,
+        (turned(sent), coefs_here[0].reshape(flat), factors_here[0].reshape(flat), increments[0]),
+        (((8, width), F32),),
+    )
     low, high = x_plus(low, 1), x_plus(high, 3)
     shared = (inputs, tanh_first, d_all, d_first, weighted, incs)
     piece = ((Z, 384, width), BF)
@@ -385,7 +407,8 @@
     parts = vmem_call(
         sum_x_kernel, place, (own, up, down, small), [((400, width), BF)] * Z
     )
-    parts = [parts[0]] + [z_plus(parts[r], r) for r in range(1, Z)]
+    arrived = {r: z_plus(parts[r], r) for r in (3, 5, 4, 2, 6, 1, 7)}
+    parts = [parts[0]] + [arrived[r] for r in range(1, Z)]
     main, far = vmem_call(
         sum_z_kernel, place, parts, (((336, width), BF), ((64, width), BF))
     )

time: 220 us -> 204 us (0.927)
  Pallas kernels: 34.8 us -> 18.9 us
    pallas_call x10 -> x11, Pallas kernels: 32.1 us -> 16 us  [vmem_call(): pl.pallas_call(kernel, out_shape=[jax.ShapeDtypeStruct(shape, dtype) for...]
    ppermute x2, starting transfers between devices: 12.4 us -> 15.2 us  [turned(): return lax.ppermute(value, ('y', 'x'), pairs)]
    unnamed x66 -> x32, local copies, waits for them, and re-layouts: 7.86 us -> 5.15 us
  transfers between devices with their start and end apart: 36 -> 36, of which waited for: 23 -> 23; matrix products, arithmetic and copies ran while one was open for 2% -> 3% of each run, Pallas kernels for 4% -> 4%
where the time goes in v1:
time: 204 us; the launch traced here: 203 us
  waiting for transfers between devices  77.5 us (38%)
  starting transfers between devices  62.5 us (31%)
  blocking collectives  26.2 us (13%)
  Pallas kernels  18.9 us (9%)
  local copies, waits for them, and re-layouts  11.1 us (5%)
  other arithmetic  4.99 us (2%)
    ppermute x28, waiting for transfers between devices, shifted(): return lax.ppermute(value, axis, [(i, (i + o) % n) for i in range(n)])  70 us
    ppermute x28, starting transfers between devices, shifted(): return lax.ppermute(value, axis, [(i, (i + o) % n) for i in range(n)])  46.5 us
    all_gather x1, blocking collectives, local(): own = lax.all_gather(pieces, 'z')  26.2 us
    pallas_call x11, Pallas kernels, vmem_call(): pl.pallas_call(kernel, out_shape=[jax.ShapeDtypeStruct(shape, dtype) for...  16 us
    ppermute x2, starting transfers between devices, turned(): return lax.ppermute(value, ('y', 'x'), pairs)  15.2 us
    unnamed x32, local copies, waits for them, and re-layouts  5.15 us
  transfers between devices with their start and end apart: 36, of which 23 were waited for; matrix products, arithmetic and copies ran while one was open for 3% of the time, Pallas kernels for 4%

profile of v1, /device:TPU:4, one launch (start us, length us, event | category | flops | bytes accessed | tf_op | source)
XLA Modules:
  0.0 203.0 jit_solution(6923531248494909871)
XLA Ops:
  3.7 2.9 %pack_kernel.1.own = bf16[3072,128]{1,0:T(8,128)(2,1)} custom-call(s32[4]{0:T(128)} %pad_add_fusion.place, bf16[4,1024,128]{2,1,0:T(8,128)(2,1)} %first.1, bf16[4,128,1024]{2,1,0:T(8,128)(2,1)} %second.1, bf16[4,2,512,128]{3,2,1,0:T(8,128)(2,1)} %bitcast.94, bf16[512,128]{1,0:T(8,128)(2,1)} %copy-done.11), custom_call_target="tpu_custom_call" | custom-call | tf_op jit(solution)/shard_map/pack_kernel/pallas_call | solution.py:314
  9.0 3.1 %collective-permute-start.3 = (bf16[2,256,128]{2,1,0:T(8,128)(2,1)S(1)}, bf16[2,256,128]{2,1,0:T(8,128)(2,1)S(1)}, u32[]{:S(2)}, u32[]{:S(2)}) collective-permute-start(bf16[2,256,128]{2,1,0:T(8,128)(2,1)S(1)} %get-tuple-element.106), channel_id=1, source_target_pairs={{0,24},{8,0},{16,8},{24,16},{1,25},{9,1},{17,9},{25,17},{2,26},{10... | collective-permute-start | bytes 393224 | tf_op jit(solution)/shard_map/ppermute | solution.py:27
  14.0 3.5 %collective-permute-done.3 = bf16[2,256,128]{2,1,0:T(8,128)(2,1)S(1)} collective-permute-done((bf16[2,256,128]{2,1,0:T(8,128)(2,1)S(1)}, bf16[2,256,128]{2,1,0:T(8,128)(2,1)S(1)}, u32[]{:S(2)}, u32[]{:S(2)}) %collective-permute-start.3) | collective-permute-done | bytes 131104 | tf_op jit(solution)/shard_map/ppermute | solution.py:27
  17.5 2.3 %collective-permute-done.2 = bf16[2,256,128]{2,1,0:T(8,128)(2,1)S(1)} collective-permute-done((bf16[2,256,128]{2,1,0:T(8,128)(2,1)S(1)}, bf16[2,256,128]{2,1,0:T(8,128)(2,1)S(1)}, u32[]{:S(2)}, u32[]{:S(2)}) %collective-permute-start.2) | collective-permute-done | bytes 131104 | tf_op jit(solution)/shard_map/ppermute | solution.py:27
  21.9 3.9 %collective-permute-start.5 = (bf16[2,256,128]{2,1,0:T(8,128)(2,1)S(1)}, bf16[2,256,128]{2,1,0:T(8,128)(2,1)S(1)}, u32[]{:S(2)}, u32[]{:S(2)}) collective-permute-start(bf16[2,256,128]{2,1,0:T(8,128)(2,1)S(1)} %get-tuple-element.104), channel_id=1, source_target_pairs={{0,4},{2,6},{4,0},{6,2},{1,5},{3,7},{5,1},{7,3},{8,12},{10,14},{12... | collective-permute-start | bytes 393224 | tf_op jit(solution)/shard_map/ppermute | solution.py:27
  25.8 4.2 %collective-permute-done.6 = bf16[2,256,128]{2,1,0:T(8,128)(2,1)S(1)} collective-permute-done((bf16[2,256,128]{2,1,0:T(8,128)(2,1)S(1)}, bf16[2,256,128]{2,1,0:T(8,128)(2,1)S(1)}, u32[]{:S(2)}, u32[]{:S(2)}) %collective-permute-start.6) | collective-permute-done | bytes 131104 | tf_op jit(solution)/shard_map/ppermute | solution.py:27
  30.1 2.2 %collective-permute-done.5 = bf16[2,256,128]{2,1,0:T(8,128)(2,1)S(1)} collective-permute-done((bf16[2,256,128]{2,1,0:T(8,128)(2,1)S(1)}, bf16[2,256,128]{2,1,0:T(8,128)(2,1)S(1)}, u32[]{:S(2)}, u32[]{:S(2)}) %collective-permute-start.5) | collective-permute-done | bytes 131104 | tf_op jit(solution)/shard_map/ppermute | solution.py:27
  36.9 7.8 %collective-permute-start.12 = (f32[4,128]{1,0:T(4,128)S(1)}, f32[4,128]{1,0:T(4,128)}, u32[]{:S(2)}, u32[]{:S(2)}) collective-permute-start(f32[4,128]{1,0:T(4,128)S(1)} %pad_maximum_fusion.3), channel_id=1, source_target_pairs={{0,0},{2,8},{4,16},{6,24},{8,2},{10,10},{12,18},{14,26},{16,4},{18... | collective-permute-start | bytes 6152 | tf_op jit(solution)/shard_map/ppermute | solution.py:48
  49.0 3.2 %shard_map.137 = (f32[256,512]{1,0:T(8,128)S(1)}, f32[256,512]{1,0:T(8,128)S(1)}, f32[256,512]{1,0:T(8,128)}) custom-call(s32[4]{0:T(128)S(1)} %copy-done.9, bf16[256,1024]{1,0:T(8,128)(2,1)S(1)} %get-tuple-element.49.in_ref, bf16[3072,128]{1,0:T(8,128)(2,1)S(1)} %copy-done, bf16[3072,128]{1,0:T(8,128)(2,1)S(1)} %collective-permute-done.8.below, ...), custom_call_target="tpu_custom_call" | custom-call | tf_op jit(solution)/shard_map/pallas_call | solution.py:65
  57.0 1.9 shard_map.138
  62.8 2.4 %collective-permute-start.17 = (f32[2,128]{1,0:T(2,128)S(1)}, f32[2,128]{1,0:T(2,128)S(1)}, u32[]{:S(2)}, u32[]{:S(2)}) collective-permute-start(f32[2,128]{1,0:T(2,128)S(1)} %add.185), channel_id=1, source_target_pairs={{0,24},{8,0},{16,8},{24,16},{1,25},{9,1},{17,9},{25,17},{2,26},{10... | collective-permute-start | bytes 3080 | tf_op jit(solution)/shard_map/ppermute | solution.py:27
  65.2 2.2 %collective-permute-start.15 = (f32[2,128]{1,0:T(2,128)S(1)}, f32[2,128]{1,0:T(2,128)S(1)}, u32[]{:S(2)}, u32[]{:S(2)}) collective-permute-start(f32[2,128]{1,0:T(2,128)S(1)} %add.185), channel_id=1, source_target_pairs={{0,16},{8,24},{16,0},{24,8},{1,17},{9,25},{17,1},{25,9},{2,18},{10... | collective-permute-start | bytes 3080 | tf_op jit(solution)/shard_map/ppermute | solution.py:27
  67.4 2.6 %collective-permute-done.16 = f32[2,128]{1,0:T(2,128)S(1)} collective-permute-done((f32[2,128]{1,0:T(2,128)S(1)}, f32[2,128]{1,0:T(2,128)S(1)}, u32[]{:S(2)}, u32[]{:S(2)}) %collective-permute-start.16) | collective-permute-done | bytes 1056 | tf_op jit(solution)/shard_map/ppermute | solution.py:27
  73.1 2.3 %shard_map.139 = (bf16[4,384,128]{2,1,0:T(8,128)(2,1)S(1)}, bf16[4,384,128]{2,1,0:T(8,128)(2,1)S(1)}, bf16[256,1024]{1,0:T(8,128)(2,1)S(1)}, bf16[256,512]{1,0:T(8,128)(2,1)S(1)}, f32[2,128]{1,0:T(2,128)S(1)}) custom-call(s32[4]{0:T(128)S(1)} %copy-done.9, bf16[256,1024]{1,0:T(8,128)(2,1)S(1)} %get-tuple-element.49.in_ref, f32[256,512]{1,0:T(8,128)S(1)} %copy-done.2, ...), custom_call_target="tpu_custom_call" | custom-call | tf_op jit(solution)/shard_map/pallas_call | solution.py:65
  77.6 7.4 %collective-permute-start.21 = (f32[2,128]{1,0:T(2,128)S(1)}, f32[2,128]{1,0:T(2,128)S(1)}, u32[]{:S(2)}, u32[]{:S(2)}) collective-permute-start(f32[2,128]{1,0:T(2,128)S(1)} %get-tuple-element.63), channel_id=1, source_target_pairs={{0,0},{2,8},{4,16},{6,24},{8,2},{10,10},{12,18},{14,26},{16,4},{18... | collective-permute-start | bytes 3080 | tf_op jit(solution)/shard_map/ppermute | solution.py:48
  86.1 3.5 %collective-permute-done.21.error = f32[2,128]{1,0:T(2,128)S(1)} collective-permute-done((f32[2,128]{1,0:T(2,128)S(1)}, f32[2,128]{1,0:T(2,128)S(1)}, u32[]{:S(2)}, u32[]{:S(2)}) %collective-permute-start.21) | collective-permute-done | bytes 1056 | tf_op jit(solution)/shard_map/ppermute | solution.py:48
  91.7 4.7 %collective-permute-start.22 = (bf16[8,384,128]{2,1,0:T(8,128)(2,1)S(1)}, bf16[8,384,128]{2,1,0:T(8,128)(2,1)S(1)}, u32[]{:S(2)}, u32[]{:S(2)}) collective-permute-start(bf16[8,384,128]{2,1,0:T(8,128)(2,1)S(1)} %get-tuple-element.64), channel_id=1, source_target_pairs={{0,2},{2,4},{4,6},{6,0},{1,3},{3,5},{5,7},{7,1},{8,10},{10,12},{12... | collective-permute-start | bytes 2359304 | tf_op jit(solution)/shard_map/ppermute | solution.py:27
  96.4 15.7 %collective-permute-done.22.from_below = bf16[8,384,128]{2,1,0:T(8,128)(2,1)S(1)} collective-permute-done((bf16[8,384,128]{2,1,0:T(8,128)(2,1)S(1)}, bf16[8,384,128]{2,1,0:T(8,128)(2,1)S(1)}, u32[]{:S(2)}, u32[]{:S(2)}) %collective-permute-start.22) | collective-permute-done | bytes 786464 | tf_op jit(solution)/shard_map/ppermute | solution.py:27
  112.1 2.2 %collective-permute-done.23.from_above = bf16[8,384,128]{2,1,0:T(8,128)(2,1)S(1)} collective-permute-done((bf16[8,384,128]{2,1,0:T(8,128)(2,1)S(1)}, bf16[8,384,128]{2,1,0:T(8,128)(2,1)S(1)}, u32[]{:S(2)}, u32[]{:S(2)}) %collective-permute-start.23) | collective-permute-done | bytes 786464 | tf_op jit(solution)/shard_map/ppermute | solution.py:27
  115.1 2.0 collective-permute-start.24
  117.1 3.3 %collective-permute-start.25 = (bf16[400,128]{1,0:T(8,128)(2,1)S(1)}, bf16[400,128]{1,0:T(8,128)(2,1)S(1)}, u32[]{:S(2)}, u32[]{:S(2)}) collective-permute-start(bf16[400,128]{1,0:T(8,128)(2,1)S(1)} %get-tuple-element.68), channel_id=1, source_target_pairs={{0,64},{32,96},{64,128},{96,160},{128,192},{160,224},{192,0},{224,... | collective-permute-start | bytes 307208 | tf_op jit(solution)/shard_map/ppermute | solution.py:27
  120.4 4.1 %collective-permute-start.26 = (bf16[400,128]{1,0:T(8,128)(2,1)S(1)}, bf16[400,128]{1,0:T(8,128)(2,1)S(1)}, u32[]{:S(2)}, u32[]{:S(2)}) collective-permute-start(bf16[400,128]{1,0:T(8,128)(2,1)S(1)} %get-tuple-element.69), channel_id=1, source_target_pairs={{0,96},{32,128},{64,160},{96,192},{128,224},{160,0},{192,32},{224,... | collective-permute-start | bytes 307208 | tf_op jit(solution)/shard_map/ppermute | solution.py:27
  125.0 4.9 %collective-permute-start.28 = (bf16[400,128]{1,0:T(8,128)(2,1)S(1)}, bf16[400,128]{1,0:T(8,128)(2,1)S(1)}, u32[]{:S(2)}, u32[]{:S(2)}) collective-permute-start(bf16[400,128]{1,0:T(8,128)(2,1)S(1)} %get-tuple-element.71), channel_id=1, source_target_pairs={{0,160},{32,192},{64,224},{96,0},{128,32},{160,64},{192,96},{224,1... | collective-permute-start | bytes 307208 | tf_op jit(solution)/shard_map/ppermute | solution.py:27
  129.9 2.7 %collective-permute-start.29 = (bf16[400,128]{1,0:T(8,128)(2,1)S(1)}, bf16[400,128]{1,0:T(8,128)(2,1)S(1)}, u32[]{:S(2)}, u32[]{:S(2)}) collective-permute-start(bf16[400,128]{1,0:T(8,128)(2,1)S(1)} %get-tuple-element.72), channel_id=1, source_target_pairs={{0,192},{32,224},{64,0},{96,32},{128,64},{160,96},{192,128},{224,1... | collective-permute-start | bytes 307208 | tf_op jit(solution)/shard_map/ppermute | solution.py:27
  134.2 2.6 %collective-permute-done.26.refs_3_ = bf16[400,128]{1,0:T(8,128)(2,1)S(1)} collective-permute-done((bf16[400,128]{1,0:T(8,128)(2,1)S(1)}, bf16[400,128]{1,0:T(8,128)(2,1)S(1)}, u32[]{:S(2)}, u32[]{:S(2)}) %collective-permute-start.26) | collective-permute-done | bytes 102432 | tf_op jit(solution)/shard_map/ppermute | solution.py:27
  136.8 3.9 %collective-permute-done.28.refs_5_ = bf16[400,128]{1,0:T(8,128)(2,1)S(1)} collective-permute-done((bf16[400,128]{1,0:T(8,128)(2,1)S(1)}, bf16[400,128]{1,0:T(8,128)(2,1)S(1)}, u32[]{:S(2)}, u32[]{:S(2)}) %collective-permute-start.28) | collective-permute-done | bytes 102432 | tf_op jit(solution)/shard_map/ppermute | solution.py:27
  140.7 1.8 collective-permute-done.29.refs_6_
  146.1 26.2 %all-gather = bf16[3200,128]{1,0:T(8,128)(2,1)S(1)} all-gather(bf16[400,128]{1,0:T(8,128)(2,1)S(1)} %shard_map.145), channel_id=2, replica_groups=mesh['z'=8,'y'=4,'x'=4,'core'=2] {'z'}, dimensions={0}, use_global_device_ids=true | all-gather | bytes 921600 | tf_op jit(solution)/shard_map/all_gather | solution.py:416
  174.4 16.3 %collective-permute-done.33.above = bf16[8,400,128]{2,1,0:T(8,128)(2,1)S(1)} collective-permute-done((bf16[8,400,128]{2,1,0:T(8,128)(2,1)S(1)}, bf16[8,400,128]{2,1,0:T(8,128)(2,1)S(1)}, u32[]{:S(2)}, u32[]{:S(2)}) %collective-permute-start.33) | collective-permute-done | bytes 819232 | tf_op jit(solution)/shard_map/ppermute | solution.py:27
  191.1 1.8 collective-permute-start.34
  192.9 5.8 %collective-permute-done.35.high = bf16[4,400,128]{2,1,0:T(8,128)(2,1)S(1)} collective-permute-done((bf16[4,400,128]{2,1,0:T(8,128)(2,1)S(1)}, bf16[4,400,128]{2,1,0:T(8,128)(2,1)S(1)}, u32[]{:S(2)}, u32[]{:S(2)}) %collective-permute-start.35) | collective-permute-done | bytes 409632 | tf_op jit(solution)/shard_map/ppermute | solution.py:27
  200.4 2.6 %shard_map.146 = (bf16[4,8,128,128]{3,2,1,0:T(8,128)(2,1)}, bf16[4,128,1024]{2,1,0:T(8,128)(2,1)}, bf16[4,2,8,64,128]{4,3,2,1,0:T(8,128)(2,1)}, f32[1,1]{1,0:T(1...) custom-call(s32[4]{0:T(128)S(1)} %copy-done.9, bf16[8,400,128]{2,1,0:T(8,128)(2,1)S(1)} %bitcast.89, ...), custom_call_target="tpu_custom_call" | custom-call | tf_op jit(solution)/shard_map/pallas_call | solution.py:65
  (118 shorter events, 45.4 us)
Async XLA Ops:
  6.6 26.7 %collective-permute-start.10 = (bf16[3072,128]{1,0:T(8,128)(2,1)}, bf16[3072,128]{1,0:T(8,128)(2,1)S(1)}, u32[]{:S(2)}, u32[]{:S(2)}) collective-permute-start(bf16[3072,128]{1,0:T(8,128)(2,1)} %pack_kernel.1.own), channel_id=1, source_target_pairs={{0,6},{2,0},{4,2},{6,4},{1,7},{3,1},{5,3},{7,5},{8,14},{10,8},{12,... | collective-permute-start | bytes 2359304 | tf_op jit(solution)/shard_map/ppermute | solution.py:27
  7.2 28.4 %collective-permute-start.8 = (bf16[3072,128]{1,0:T(8,128)(2,1)}, bf16[3072,128]{1,0:T(8,128)(2,1)S(1)}, u32[]{:S(2)}, u32[]{:S(2)}) collective-permute-start(bf16[3072,128]{1,0:T(8,128)(2,1)} %pack_kernel.1.own), channel_id=1, source_target_pairs={{0,2},{2,4},{4,6},{6,0},{1,3},{3,5},{5,7},{7,1},{8,10},{10,12},{12... | collective-permute-start | bytes 2359304 | tf_op jit(solution)/shard_map/ppermute | solution.py:27
  9.0 8.4 %collective-permute-start.3 = (bf16[2,256,128]{2,1,0:T(8,128)(2,1)S(1)}, bf16[2,256,128]{2,1,0:T(8,128)(2,1)S(1)}, u32[]{:S(2)}, u32[]{:S(2)}) collective-permute-start(bf16[2,256,128]{2,1,0:T(8,128)(2,1)S(1)} %get-tuple-element.106), channel_id=1, source_target_pairs={{0,24},{8,0},{16,8},{24,16},{1,25},{9,1},{17,9},{25,17},{2,26},{10... | collective-permute-start | bytes 393224 | tf_op jit(solution)/shard_map/ppermute | solution.py:27
  12.1 7.6 %collective-permute-start.2 = (bf16[2,256,128]{2,1,0:T(8,128)(2,1)S(1)}, bf16[2,256,128]{2,1,0:T(8,128)(2,1)S(1)}, u32[]{:S(2)}, u32[]{:S(2)}) collective-permute-start(bf16[2,256,128]{2,1,0:T(8,128)(2,1)S(1)} %get-tuple-element.107), channel_id=1, source_target_pairs={{0,16},{8,24},{16,0},{24,8},{1,17},{9,25},{17,1},{25,9},{2,18},{10... | collective-permute-start | bytes 393224 | tf_op jit(solution)/shard_map/ppermute | solution.py:27
  12.8 8.4 %collective-permute-start.1 = (bf16[2,256,128]{2,1,0:T(8,128)(2,1)S(1)}, bf16[2,256,128]{2,1,0:T(8,128)(2,1)S(1)}, u32[]{:S(2)}, u32[]{:S(2)}) collective-permute-start(bf16[2,256,128]{2,1,0:T(8,128)(2,1)S(1)} %get-tuple-element.108), channel_id=1, source_target_pairs={{0,8},{8,16},{16,24},{24,0},{1,9},{9,17},{17,25},{25,1},{2,10},{10... | collective-permute-start | bytes 393224 | tf_op jit(solution)/shard_map/ppermute | solution.py:27
  21.3 8.8 %collective-permute-start.6 = (bf16[2,256,128]{2,1,0:T(8,128)(2,1)S(1)}, bf16[2,256,128]{2,1,0:T(8,128)(2,1)S(1)}, u32[]{:S(2)}, u32[]{:S(2)}) collective-permute-start(bf16[2,256,128]{2,1,0:T(8,128)(2,1)S(1)} %get-tuple-element.103), channel_id=1, source_target_pairs={{0,6},{2,0},{4,2},{6,4},{1,7},{3,1},{5,3},{7,5},{8,14},{10,8},{12,... | collective-permute-start | bytes 393224 | tf_op jit(solution)/shard_map/ppermute | solution.py:27
  21.9 10.4 %collective-permute-start.5 = (bf16[2,256,128]{2,1,0:T(8,128)(2,1)S(1)}, bf16[2,256,128]{2,1,0:T(8,128)(2,1)S(1)}, u32[]{:S(2)}, u32[]{:S(2)}) collective-permute-start(bf16[2,256,128]{2,1,0:T(8,128)(2,1)S(1)} %get-tuple-element.104), channel_id=1, source_target_pairs={{0,4},{2,6},{4,0},{6,2},{1,5},{3,7},{5,1},{7,3},{8,12},{10,14},{12... | collective-permute-start | bytes 393224 | tf_op jit(solution)/shard_map/ppermute | solution.py:27
  25.8 7.2 %collective-permute-start.4 = (bf16[2,256,128]{2,1,0:T(8,128)(2,1)S(1)}, bf16[2,256,128]{2,1,0:T(8,128)(2,1)S(1)}, u32[]{:S(2)}, u32[]{:S(2)}) collective-permute-start(bf16[2,256,128]{2,1,0:T(8,128)(2,1)S(1)} %get-tuple-element.105), channel_id=1, source_target_pairs={{0,2},{2,4},{4,6},{6,0},{1,3},{3,5},{5,7},{7,1},{8,10},{10,12},{12... | collective-permute-start | bytes 393224 | tf_op jit(solution)/shard_map/ppermute | solution.py:27
  33.1 12.1 %collective-permute-start.7 = (bf16[4,2,256,128]{3,2,1,0:T(8,128)(2,1)S(1)}, bf16[4,2,256,128]{3,2,1,0:T(8,128)(2,1)S(1)}, u32[]{:S(2)}, u32[]{:S(2)}) collective-permute-start(bf16[4,2,256,128]{3,2,1,0:T(8,128)(2,1)S(1)} %pad_maximum_fusion.2.near), channel_id=1, source_target_pairs={{0,1},{1,0},{2,3},{3,2},{4,5},{5,4},{6,7},{7,6},{8,9},{9,8},{10,11... | collective-permute-start | bytes 1572872 | tf_op jit(solution)/shard_map/ppermute | solution.py:31
  34.0 14.9 %collective-permute-start.11 = (bf16[1536,128]{1,0:T(8,128)(2,1)}, bf16[1536,128]{1,0:T(8,128)(2,1)}, u32[]{:S(2)}, u32[]{:S(2)}) collective-permute-start(bf16[1536,128]{1,0:T(8,128)(2,1)} %slice.95), channel_id=1, source_target_pairs={{0,6},{2,0},{4,2},{6,4},{1,7},{3,1},{5,3},{7,5},{8,14},{10,8},{12,... | collective-permute-start | bytes 1179656 | tf_op jit(solution)/shard_map/ppermute | solution.py:27
  36.4 12.6 %collective-permute-start.9 = (bf16[1536,128]{1,0:T(8,128)(2,1)}, bf16[1536,128]{1,0:T(8,128)(2,1)}, u32[]{:S(2)}, u32[]{:S(2)}) collective-permute-start(bf16[1536,128]{1,0:T(8,128)(2,1)} %slice.94), channel_id=1, source_target_pairs={{0,2},{2,4},{4,6},{6,0},{1,3},{3,5},{5,7},{7,1},{8,10},{10,12},{12... | collective-permute-start | bytes 1179656 | tf_op jit(solution)/shard_map/ppermute | solution.py:27
  36.9 17.0 %collective-permute-start.12 = (f32[4,128]{1,0:T(4,128)S(1)}, f32[4,128]{1,0:T(4,128)}, u32[]{:S(2)}, u32[]{:S(2)}) collective-permute-start(f32[4,128]{1,0:T(4,128)S(1)} %pad_maximum_fusion.3), channel_id=1, source_target_pairs={{0,0},{2,8},{4,16},{6,24},{8,2},{10,10},{12,18},{14,26},{16,4},{18... | collective-permute-start | bytes 6152 | tf_op jit(solution)/shard_map/ppermute | solution.py:48
  54.5 5.1 %collective-permute-start.13 = (f32[256,512]{1,0:T(8,128)}, f32[256,512]{1,0:T(8,128)}, u32[]{:S(2)}, u32[]{:S(2)}) collective-permute-start(f32[256,512]{1,0:T(8,128)} %get-tuple-element.55), channel_id=1, source_target_pairs={{0,1},{1,0},{2,3},{3,2},{4,5},{5,4},{6,7},{7,6},{8,9},{9,8},{10,11... | collective-permute-start | bytes 1572872 | tf_op jit(solution)/shard_map/ppermute | solution.py:31
  62.8 4.6 %collective-permute-start.17 = (f32[2,128]{1,0:T(2,128)S(1)}, f32[2,128]{1,0:T(2,128)S(1)}, u32[]{:S(2)}, u32[]{:S(2)}) collective-permute-start(f32[2,128]{1,0:T(2,128)S(1)} %add.185), channel_id=1, source_target_pairs={{0,24},{8,0},{16,8},{24,16},{1,25},{9,1},{17,9},{25,17},{2,26},{10... | collective-permute-start | bytes 3080 | tf_op jit(solution)/shard_map/ppermute | solution.py:27
  65.2 4.8 %collective-permute-start.16 = (f32[2,128]{1,0:T(2,128)S(1)}, f32[2,128]{1,0:T(2,128)S(1)}, u32[]{:S(2)}, u32[]{:S(2)}) collective-permute-start(f32[2,128]{1,0:T(2,128)S(1)} %add.185), channel_id=1, source_target_pairs={{0,8},{8,16},{16,24},{24,0},{1,9},{9,17},{17,25},{25,1},{2,10},{10... | collective-permute-start | bytes 3080 | tf_op jit(solution)/shard_map/ppermute | solution.py:27
  65.2 5.1 %collective-permute-start.15 = (f32[2,128]{1,0:T(2,128)S(1)}, f32[2,128]{1,0:T(2,128)S(1)}, u32[]{:S(2)}, u32[]{:S(2)}) collective-permute-start(f32[2,128]{1,0:T(2,128)S(1)} %add.185), channel_id=1, source_target_pairs={{0,16},{8,24},{16,0},{24,8},{1,17},{9,25},{17,1},{25,9},{2,18},{10... | collective-permute-start | bytes 3080 | tf_op jit(solution)/shard_map/ppermute | solution.py:27
  75.5 14.9 %collective-permute-start.19 = (bf16[4,384,128]{2,1,0:T(8,128)(2,1)S(1)}, bf16[4,384,128]{2,1,0:T(8,128)(2,1)S(1)}, u32[]{:S(2)}, u32[]{:S(2)}) collective-permute-start(bf16[4,384,128]{2,1,0:T(8,128)(2,1)S(1)} %get-tuple-element.60), channel_id=1, source_target_pairs={{0,2},{2,4},{4,6},{6,0},{1,3},{3,5},{5,7},{7,1},{8,10},{10,12},{12... | collective-permute-start | bytes 1179656 | tf_op jit(solution)/shard_map/ppermute | solution.py:27
  76.2 14.2 %collective-permute-start.20 = (bf16[4,384,128]{2,1,0:T(8,128)(2,1)S(1)}, bf16[4,384,128]{2,1,0:T(8,128)(2,1)S(1)}, u32[]{:S(2)}, u32[]{:S(2)}) collective-permute-start(bf16[4,384,128]{2,1,0:T(8,128)(2,1)S(1)} %get-tuple-element.61), channel_id=1, source_target_pairs={{0,6},{2,0},{4,2},{6,4},{1,7},{3,1},{5,3},{7,5},{8,14},{10,8},{12,... | collective-permute-start | bytes 1179656 | tf_op jit(solution)/shard_map/ppermute | solution.py:27
  77.6 12.0 %collective-permute-start.21 = (f32[2,128]{1,0:T(2,128)S(1)}, f32[2,128]{1,0:T(2,128)S(1)}, u32[]{:S(2)}, u32[]{:S(2)}) collective-permute-start(f32[2,128]{1,0:T(2,128)S(1)} %get-tuple-element.63), channel_id=1, source_target_pairs={{0,0},{2,8},{4,16},{6,24},{8,2},{10,10},{12,18},{14,26},{16,4},{18... | collective-permute-start | bytes 3080 | tf_op jit(solution)/shard_map/ppermute | solution.py:48
  91.7 20.4 %collective-permute-start.22 = (bf16[8,384,128]{2,1,0:T(8,128)(2,1)S(1)}, bf16[8,384,128]{2,1,0:T(8,128)(2,1)S(1)}, u32[]{:S(2)}, u32[]{:S(2)}) collective-permute-start(bf16[8,384,128]{2,1,0:T(8,128)(2,1)S(1)} %get-tuple-element.64), channel_id=1, source_target_pairs={{0,2},{2,4},{4,6},{6,0},{1,3},{3,5},{5,7},{7,1},{8,10},{10,12},{12... | collective-permute-start | bytes 2359304 | tf_op jit(solution)/shard_map/ppermute | solution.py:27
  96.4 17.9 %collective-permute-start.23 = (bf16[8,384,128]{2,1,0:T(8,128)(2,1)S(1)}, bf16[8,384,128]{2,1,0:T(8,128)(2,1)S(1)}, u32[]{:S(2)}, u32[]{:S(2)}) collective-permute-start(bf16[8,384,128]{2,1,0:T(8,128)(2,1)S(1)} %get-tuple-element.65), channel_id=1, source_target_pairs={{0,6},{2,0},{4,2},{6,4},{1,7},{3,1},{5,3},{7,5},{8,14},{10,8},{12,... | collective-permute-start | bytes 2359304 | tf_op jit(solution)/shard_map/ppermute | solution.py:27
  115.1 14.8 %collective-permute-start.24 = (bf16[400,128]{1,0:T(8,128)(2,1)S(1)}, bf16[400,128]{1,0:T(8,128)(2,1)S(1)}, u32[]{:S(2)}, u32[]{:S(2)}) collective-permute-start(bf16[400,128]{1,0:T(8,128)(2,1)S(1)} %get-tuple-element.67), channel_id=1, source_target_pairs={{0,32},{32,64},{64,96},{96,128},{128,160},{160,192},{192,224},{224... | collective-permute-start | bytes 307208 | tf_op jit(solution)/shard_map/ppermute | solution.py:27
  117.1 17.1 %collective-permute-start.25 = (bf16[400,128]{1,0:T(8,128)(2,1)S(1)}, bf16[400,128]{1,0:T(8,128)(2,1)S(1)}, u32[]{:S(2)}, u32[]{:S(2)}) collective-permute-start(bf16[400,128]{1,0:T(8,128)(2,1)S(1)} %get-tuple-element.68), channel_id=1, source_target_pairs={{0,64},{32,96},{64,128},{96,160},{128,192},{160,224},{192,0},{224,... | collective-permute-start | bytes 307208 | tf_op jit(solution)/shard_map/ppermute | solution.py:27
  120.4 16.4 %collective-permute-start.26 = (bf16[400,128]{1,0:T(8,128)(2,1)S(1)}, bf16[400,128]{1,0:T(8,128)(2,1)S(1)}, u32[]{:S(2)}, u32[]{:S(2)}) collective-permute-start(bf16[400,128]{1,0:T(8,128)(2,1)S(1)} %get-tuple-element.69), channel_id=1, source_target_pairs={{0,96},{32,128},{64,160},{96,192},{128,224},{160,0},{192,32},{224,... | collective-permute-start | bytes 307208 | tf_op jit(solution)/shard_map/ppermute | solution.py:27
  124.4 12.4 %collective-permute-start.27 = (bf16[400,128]{1,0:T(8,128)(2,1)S(1)}, bf16[400,128]{1,0:T(8,128)(2,1)S(1)}, u32[]{:S(2)}, u32[]{:S(2)}) collective-permute-start(bf16[400,128]{1,0:T(8,128)(2,1)S(1)} %get-tuple-element.70), channel_id=1, source_target_pairs={{0,128},{32,160},{64,192},{96,224},{128,0},{160,32},{192,64},{224,... | collective-permute-start | bytes 307208 | tf_op jit(solution)/shard_map/ppermute | solution.py:27
  125.0 15.7 %collective-permute-start.28 = (bf16[400,128]{1,0:T(8,128)(2,1)S(1)}, bf16[400,128]{1,0:T(8,128)(2,1)S(1)}, u32[]{:S(2)}, u32[]{:S(2)}) collective-permute-start(bf16[400,128]{1,0:T(8,128)(2,1)S(1)} %get-tuple-element.71), channel_id=1, source_target_pairs={{0,160},{32,192},{64,224},{96,0},{128,32},{160,64},{192,96},{224,1... | collective-permute-start | bytes 307208 | tf_op jit(solution)/shard_map/ppermute | solution.py:27
  129.9 12.6 %collective-permute-start.29 = (bf16[400,128]{1,0:T(8,128)(2,1)S(1)}, bf16[400,128]{1,0:T(8,128)(2,1)S(1)}, u32[]{:S(2)}, u32[]{:S(2)}) collective-permute-start(bf16[400,128]{1,0:T(8,128)(2,1)S(1)} %get-tuple-element.72), channel_id=1, source_target_pairs={{0,192},{32,224},{64,0},{96,32},{128,64},{160,96},{192,128},{224,1... | collective-permute-start | bytes 307208 | tf_op jit(solution)/shard_map/ppermute | solution.py:27
  134.2 9.4 %collective-permute-start.30 = (bf16[400,128]{1,0:T(8,128)(2,1)S(1)}, bf16[400,128]{1,0:T(8,128)(2,1)S(1)}, u32[]{:S(2)}, u32[]{:S(2)}) collective-permute-start(bf16[400,128]{1,0:T(8,128)(2,1)S(1)} %get-tuple-element.73), channel_id=1, source_target_pairs={{0,224},{32,0},{64,32},{96,64},{128,96},{160,128},{192,160},{224,1... | collective-permute-start | bytes 307208 | tf_op jit(solution)/shard_map/ppermute | solution.py:27
  172.3 18.3 %collective-permute-start.33 = (bf16[8,400,128]{2,1,0:T(8,128)(2,1)S(1)}, bf16[8,400,128]{2,1,0:T(8,128)(2,1)S(1)}, u32[]{:S(2)}, u32[]{:S(2)}) collective-permute-start(bf16[8,400,128]{2,1,0:T(8,128)(2,1)S(1)} %bitcast.87), channel_id=1, source_target_pairs={{0,24},{8,0},{16,8},{24,16},{1,25},{9,1},{17,9},{25,17},{2,26},{10... | collective-permute-start | bytes 2457608 | tf_op jit(solution)/shard_map/ppermute | solution.py:27
  172.7 18.4 %collective-permute-start.32 = (bf16[8,400,128]{2,1,0:T(8,128)(2,1)S(1)}, bf16[8,400,128]{2,1,0:T(8,128)(2,1)S(1)}, u32[]{:S(2)}, u32[]{:S(2)}) collective-permute-start(bf16[8,400,128]{2,1,0:T(8,128)(2,1)S(1)} %bitcast.88), channel_id=1, source_target_pairs={{0,8},{8,16},{16,24},{24,0},{1,9},{9,17},{17,25},{25,1},{2,10},{10... | collective-permute-start | bytes 2457608 | tf_op jit(solution)/shard_map/ppermute | solution.py:27
  190.7 8.0 %collective-permute-start.35 = (bf16[4,400,128]{2,1,0:T(8,128)(2,1)S(1)}, bf16[4,400,128]{2,1,0:T(8,128)(2,1)S(1)}, u32[]{:S(2)}, u32[]{:S(2)}) collective-permute-start(bf16[4,400,128]{2,1,0:T(8,128)(2,1)S(1)} %slice.103), channel_id=1, source_target_pairs={{0,24},{8,0},{16,8},{24,16},{1,25},{9,1},{17,9},{25,17},{2,26},{10... | collective-permute-start | bytes 1228808 | tf_op jit(solution)/shard_map/ppermute | solution.py:27
  191.1 9.2 %collective-permute-start.34 = (bf16[4,400,128]{2,1,0:T(8,128)(2,1)S(1)}, bf16[4,400,128]{2,1,0:T(8,128)(2,1)S(1)}, u32[]{:S(2)}, u32[]{:S(2)}) collective-permute-start(bf16[4,400,128]{2,1,0:T(8,128)(2,1)S(1)} %slice.102), channel_id=1, source_target_pairs={{0,8},{8,16},{16,24},{24,0},{1,9},{9,17},{17,25},{25,1},{2,10},{10... | collective-permute-start | bytes 1228808 | tf_op jit(solution)/shard_map/ppermute | solution.py:27
  (20 other events, 48.6 us)

commit v2 on v1

--- a/solution.py
+++ b/solution.py
@@ -17,6 +17,7 @@
 DEFAULT_LOSS = 1.0 / 3.0
 
 X, CORES, Y, Z = 4, 2, 4, 8
+STEPS = 5
 W = D // (X * CORES)
 ROOM = 20 << 20
 BF = jnp.bfloat16
@@ -142,6 +143,46 @@
             at = W * (CORES * o + i)
             more = dot(inc_ref[:, at : at + W], piece, ((1,), (1,)))
             out[...] = more if i + o == 0 else out[...] + more
+
+
+def loss_kernel(place, mine, other, back, there, tanh_ref, total, coef_ref):
+    tanh = jnp.tanh(mine[...] + other[...])
+    tanh_ref[...] = tanh
+    sums = lax.dot_general(
+        jnp.ones((8, tanh.shape[1]), F32),
+        tanh * back[...],
+        (((1,), (1,)), ((), ())),
+        precision=lax.Precision.HIGHEST,
+        preferred_element_type=F32,
+    )
+    row = lax.broadcasted_iota(jnp.int32, (2, W), 0)
+    dots = jnp.where(row == 0, sums[:2, :W], sums[:2, W:])
+    step = there[2:4, :]
+    coef = jnp.ones((2, W), F32)
+    for n in range(STEPS - 1, 1, -1):
+        factor = 1.0 + DISCOUNT / STEPS - DEFAULT_LOSS * jnp.where(step == float(n), 1.0, 0.0)
+        coef = jnp.where(place[2] + 1 < n, coef * factor, coef)
+    coef_ref[...] = coef
+    total[...] = there[:2, :] + coef * dots
+
+
+def add_kernel(place, a, b, out):
+    out[...] = a[...] + b[...]
+
+
+def weigh_kernel(place, own, p1, p2, p3, coef, tanh_ref, back, weighted, d_second, error):
+    scale = 1.0 / math.sqrt(tanh_ref.shape[0] * Y * Z)
+    err = (own[...] + p2[...]) + (p1[...] + p3[...])
+    error[...] = err
+    adjoint = 2.0 * scale * err * coef[...]
+    for i in range(2):
+        at = slice(W * i, W * i + W)
+        column = jnp.transpose(jnp.broadcast_to(adjoint[i : i + 1, :], (W, W)))
+        for q in range(0, tanh_ref.shape[1], W):
+            tanh = tanh_ref[at, q : q + W]
+            weighted[at, q : q + W] = (column * tanh).astype(BF)
+            more = column * back[at, q : q + W] * (1.0 - tanh * tanh)
+            d_second[at, q : q + W] = more.astype(BF)
 
 
 def put_sums(outs, o, in_ref, tanh_ref, all_ref, d1_ref, wt_ref, inc_ref, added=None):
@@ -302,7 +343,6 @@
 ):
     steps, paths, width = increments.shape
     tstep = 1.0 / steps
-    scale = 1.0 / math.sqrt(paths * Y * Z)
     x, c, y, z = (lax.axis_index(name) for name in ("x", "core", "y", "z"))
     place = jnp.stack([x, c, y, z]).astype(jnp.int32)
     half = D // CORES
@@ -332,8 +372,9 @@
     factors_here, coefs_here = factors_of(step_here, steps)
     target_part = jnp.sum(states * term_weight[None, :], axis=1) / math.sqrt(D)
     first_part = jnp.sum(increments[0] * z_start[None, :], axis=1)
+    start = factors_here[0] * coefs_here[0] * y_start / (X * CORES)
     there = jnp.concatenate(
-        [(coefs_here[0] * first_part - target_part).reshape(flat), step_here.reshape(flat)]
+        [(coefs_here[0] * first_part - target_part + start).reshape(flat), step_here.reshape(flat)]
     )
     rows, there = lax.optimization_barrier((rows, there))
     rows = jnp.stack(rows)
@@ -358,29 +399,28 @@
         [((paths, half), F32)] * 3,
         [pltpu.VMEM((paths, D), F32)],
     )
-    there, _ = lax.optimization_barrier((there, mine))
-    part_sum = there[:2]
-    factors, coefs = factors_of(there[2:].reshape(paths), steps)
     other = core_swap(other)
     (back,) = vmem_call(back_kernel, place, (incs, *weights), [((paths, half), F32)])
-    tanh_second = jnp.tanh(mine + other)
-    dots = jnp.sum(tanh_second * back, axis=1)
-    coef = pick(coefs, y + 1)
-    total = part_sum + (coef * dots).reshape(flat)
-    total = total + core_swap(total)
+    tanh_second, total, coef = vmem_call(
+        loss_kernel,
+        place,
+        (mine, other, back, there),
+        (((paths, half), F32), (flat, F32), (flat, F32)),
+    )
+    (total,) = vmem_call(add_kernel, place, (total, core_swap(total)), ((flat, F32),))
     others = [y_plus(total, r) for r in range(1, Y)]
-    total = (total + others[1]) + (others[0] + others[2])
-    total = total + (factors[0] * coefs[0] * y_start).reshape(flat)
-    adjoint = 2.0 * scale * total.reshape(paths)
-
-    weight = (adjoint * coef)[:, None]
-    weighted = (weight * tanh_second).astype(BF)
-    d_second = (weight * back * (1.0 - tanh_second * tanh_second)).astype(BF)
+
+    weighted, d_second, error = vmem_call(
+        weigh_kernel,
+        place,
+        (total, *others, coef, tanh_second, back),
+        (((paths, half), BF), ((paths, half), BF), (flat, F32)),
+    )
     d_far = core_swap(d_second)
     low, high, d_all, d_first, sent = vmem_call(
         far_kernel,
         place,
-        (inputs, tanh_first, d_second, d_far, *weights, weighted, incs, total),
+        (inputs, tanh_first, d_second, d_far, *weights, weighted, incs, error),
         (
             ((Z // 2, 384, width), BF),
             ((Z // 2, 384, width), BF),
@@ -407,7 +447,9 @@
     parts = vmem_call(
         sum_x_kernel, place, (own, up, down, small), [((400, width), BF)] * Z
     )
-    arrived = {r: z_plus(parts[r], r) for r in (3, 5, 4, 2, 6, 1, 7)}
+    arrived = {}
+    for r in range(1, Z):
+        arrived[r] = z_plus(parts[r], r)
     parts = [parts[0]] + [arrived[r] for r in range(1, Z)]
     main, far = vmem_call(
         sum_z_kernel, place, parts, (((336, width), BF), ((64, width), BF))

time: 204 us -> 202 us (level)
  waiting for transfers between devices: 77.5 us -> 92.2 us
  local copies, waits for them, and re-layouts: 11.1 us -> 1.85 us
  starting transfers between devices: 62.5 us -> 58.2 us
  other arithmetic: 4.99 us -> 1.18 us
    ppermute x28, waiting for transfers between devices: 70 us -> 83.5 us  [shifted(): return lax.ppermute(value, axis, [(i, (i + o) % n) for i in range(n)])]
    unnamed x32 -> x16, local copies, waits for them, and re-layouts: 5.15 us -> 0.69 us
    ppermute x28, starting transfers between devices: 46.5 us -> 43.5 us  [shifted(): return lax.ppermute(value, axis, [(i, (i + o) % n) for i in range(n)])]
    pallas_call x11 -> x14, Pallas kernels: 16 us -> 15.8 us  [vmem_call(): pl.pallas_call(kernel, out_shape=[jax.ShapeDtypeStruct(shape, dtype) for...]
  transfers between devices with their start and end apart: 36 -> 36, of which waited for: 23 -> 26; matrix products, arithmetic and copies ran while one was open for 3% -> 1% of each run, Pallas kernels for 4% -> 2%
where the time goes in v2:
time: 202 us; the launch traced here: 200 us
  waiting for transfers between devices  92.2 us (46%)
  starting transfers between devices  58.2 us (29%)
  blocking collectives  26.2 us (13%)
  Pallas kernels  18.7 us (9%)
    ppermute x28, waiting for transfers between devices, shifted(): return lax.ppermute(value, axis, [(i, (i + o) % n) for i in range(n)])  83.5 us
    ppermute x28, starting transfers between devices, shifted(): return lax.ppermute(value, axis, [(i, (i + o) % n) for i in range(n)])  43.5 us
    all_gather x1, blocking collectives, local(): own = lax.all_gather(pieces, 'z')  26.2 us
    pallas_call x14, Pallas kernels, vmem_call(): pl.pallas_call(kernel, out_shape=[jax.ShapeDtypeStruct(shape, dtype) for...  15.8 us
    ppermute x2, starting transfers between devices, turned(): return lax.ppermute(value, ('y', 'x'), pairs)  14.3 us
    ppermute x2, waiting for transfers between devices, turned(): return lax.ppermute(value, ('y', 'x'), pairs)  4.76 us
  transfers between devices with their start and end apart: 36, of which 26 were waited for; matrix products, arithmetic and copies ran while one was open for 1% of the time, Pallas kernels for 2%

profile of v2, /device:TPU:4, one launch (start us, length us, event | category | flops | bytes accessed | tf_op | source)
XLA Modules:
  0.0 200.1 jit_solution(8712685894173082217)
XLA Ops:
  3.7 2.9 %pack_kernel.1.own = bf16[3072,128]{1,0:T(8,128)(2,1)} custom-call(s32[4]{0:T(128)} %pad_add_fusion.place, bf16[4,1024,128]{2,1,0:T(8,128)(2,1)} %first.1, bf16[4,128,1024]{2,1,0:T(8,128)(2,1)} %second.1, bf16[4,2,512,128]{3,2,1,0:T(8,128)(2,1)} %bitcast.86, bf16[512,128]{1,0:T(8,128)(2,1)} %copy-done.3), custom_call_target="tpu_custom_call" | custom-call | tf_op jit(solution)/shard_map/pack_kernel/pallas_call | solution.py:354
  9.1 3.1 %collective-permute-start.3 = (bf16[2,256,128]{2,1,0:T(8,128)(2,1)S(1)}, bf16[2,256,128]{2,1,0:T(8,128)(2,1)S(1)}, u32[]{:S(2)}, u32[]{:S(2)}) collective-permute-start(bf16[2,256,128]{2,1,0:T(8,128)(2,1)S(1)} %get-tuple-element.108), channel_id=1, source_target_pairs={{0,24},{8,0},{16,8},{24,16},{1,25},{9,1},{17,9},{25,17},{2,26},{10... | collective-permute-start | bytes 393224 | tf_op jit(solution)/shard_map/ppermute | solution.py:28
  14.0 3.8 %collective-permute-done.3 = bf16[2,256,128]{2,1,0:T(8,128)(2,1)S(1)} collective-permute-done((bf16[2,256,128]{2,1,0:T(8,128)(2,1)S(1)}, bf16[2,256,128]{2,1,0:T(8,128)(2,1)S(1)}, u32[]{:S(2)}, u32[]{:S(2)}) %collective-permute-start.3) | collective-permute-done | bytes 131104 | tf_op jit(solution)/shard_map/ppermute | solution.py:28
  17.8 2.2 %collective-permute-done.2 = bf16[2,256,128]{2,1,0:T(8,128)(2,1)S(1)} collective-permute-done((bf16[2,256,128]{2,1,0:T(8,128)(2,1)S(1)}, bf16[2,256,128]{2,1,0:T(8,128)(2,1)S(1)}, u32[]{:S(2)}, u32[]{:S(2)}) %collective-permute-start.2) | collective-permute-done | bytes 131104 | tf_op jit(solution)/shard_map/ppermute | solution.py:28
  22.3 3.9 %collective-permute-start.5 = (bf16[2,256,128]{2,1,0:T(8,128)(2,1)S(1)}, bf16[2,256,128]{2,1,0:T(8,128)(2,1)S(1)}, u32[]{:S(2)}, u32[]{:S(2)}) collective-permute-start(bf16[2,256,128]{2,1,0:T(8,128)(2,1)S(1)} %get-tuple-element.106), channel_id=1, source_target_pairs={{0,4},{2,6},{4,0},{6,2},{1,5},{3,7},{5,1},{7,3},{8,12},{10,14},{12... | collective-permute-start | bytes 393224 | tf_op jit(solution)/shard_map/ppermute | solution.py:28
  26.2 3.9 %collective-permute-done.6 = bf16[2,256,128]{2,1,0:T(8,128)(2,1)S(1)} collective-permute-done((bf16[2,256,128]{2,1,0:T(8,128)(2,1)S(1)}, bf16[2,256,128]{2,1,0:T(8,128)(2,1)S(1)}, u32[]{:S(2)}, u32[]{:S(2)}) %collective-permute-start.6) | collective-permute-done | bytes 131104 | tf_op jit(solution)/shard_map/ppermute | solution.py:28
  30.1 2.3 %collective-permute-done.5 = bf16[2,256,128]{2,1,0:T(8,128)(2,1)S(1)} collective-permute-done((bf16[2,256,128]{2,1,0:T(8,128)(2,1)S(1)}, bf16[2,256,128]{2,1,0:T(8,128)(2,1)S(1)}, u32[]{:S(2)}, u32[]{:S(2)}) %collective-permute-start.5) | collective-permute-done | bytes 131104 | tf_op jit(solution)/shard_map/ppermute | solution.py:28
  37.1 8.5 %collective-permute-done.11.high.w_high = bf16[1536,128]{1,0:T(8,128)(2,1)S(1)} collective-permute-done((bf16[1536,128]{1,0:T(8,128)(2,1)S(1)}, bf16[1536,128]{1,0:T(8,128)(2,1)S(1)}, u32[]{:S(2)}, u32[]{:S(2)}) %collective-permute-start.11) | collective-permute-done | bytes 393248 | tf_op jit(solution)/shard_map/ppermute | solution.py:28
  47.1 1.8 shard_map.137
  49.1 7.4 %collective-permute-start.13 = (f32[4,128]{1,0:T(4,128)S(1)}, f32[4,128]{1,0:T(4,128)S(1)}, u32[]{:S(2)}, u32[]{:S(2)}) collective-permute-start(f32[4,128]{1,0:T(4,128)S(1)} %pad_maximum_fusion.3), channel_id=1, source_target_pairs={{0,0},{2,8},{4,16},{6,24},{8,2},{10,10},{12,18},{14,26},{16,4},{18... | collective-permute-start | bytes 6152 | tf_op jit(solution)/shard_map/ppermute | solution.py:49
  70.0 1.7 shard_map.142
  71.7 3.0 %collective-permute-start.19 = (bf16[4,384,128]{2,1,0:T(8,128)(2,1)S(1)}, bf16[4,384,128]{2,1,0:T(8,128)(2,1)S(1)}, u32[]{:S(2)}, u32[]{:S(2)}) collective-permute-start(bf16[4,384,128]{2,1,0:T(8,128)(2,1)S(1)} %get-tuple-element.70), channel_id=1, source_target_pairs={{0,2},{2,4},{4,6},{6,0},{1,3},{3,5},{5,7},{7,1},{8,10},{10,12},{12... | collective-permute-start | bytes 1179656 | tf_op jit(solution)/shard_map/ppermute | solution.py:28
  75.5 6.9 %collective-permute-start.21 = (f32[2,128]{1,0:T(2,128)S(1)}, f32[2,128]{1,0:T(2,128)S(1)}, u32[]{:S(2)}, u32[]{:S(2)}) collective-permute-start(f32[2,128]{1,0:T(2,128)S(1)} %get-tuple-element.73), channel_id=1, source_target_pairs={{0,0},{2,8},{4,16},{6,24},{8,2},{10,10},{12,18},{14,26},{16,4},{18... | collective-permute-start | bytes 3080 | tf_op jit(solution)/shard_map/ppermute | solution.py:49
  83.4 4.0 %collective-permute-done.21.error = f32[2,128]{1,0:T(2,128)S(1)} collective-permute-done((f32[2,128]{1,0:T(2,128)S(1)}, f32[2,128]{1,0:T(2,128)S(1)}, u32[]{:S(2)}, u32[]{:S(2)}) %collective-permute-start.21) | collective-permute-done | bytes 1056 | tf_op jit(solution)/shard_map/ppermute | solution.py:49
  89.6 2.4 %collective-permute-start.22 = (bf16[8,384,128]{2,1,0:T(8,128)(2,1)S(1)}, bf16[8,384,128]{2,1,0:T(8,128)(2,1)S(1)}, u32[]{:S(2)}, u32[]{:S(2)}) collective-permute-start(bf16[8,384,128]{2,1,0:T(8,128)(2,1)S(1)} %get-tuple-element.74), channel_id=1, source_target_pairs={{0,2},{2,4},{4,6},{6,0},{1,3},{3,5},{5,7},{7,1},{8,10},{10,12},{12... | collective-permute-start | bytes 2359304 | tf_op jit(solution)/shard_map/ppermute | solution.py:28
  92.0 16.1 %collective-permute-done.22.from_below = bf16[8,384,128]{2,1,0:T(8,128)(2,1)S(1)} collective-permute-done((bf16[8,384,128]{2,1,0:T(8,128)(2,1)S(1)}, bf16[8,384,128]{2,1,0:T(8,128)(2,1)S(1)}, u32[]{:S(2)}, u32[]{:S(2)}) %collective-permute-start.22) | collective-permute-done | bytes 786464 | tf_op jit(solution)/shard_map/ppermute | solution.py:28
  108.1 1.8 collective-permute-done.23.from_above
  110.7 2.0 collective-permute-start.24
  112.7 3.3 %collective-permute-start.25 = (bf16[400,128]{1,0:T(8,128)(2,1)S(1)}, bf16[400,128]{1,0:T(8,128)(2,1)S(1)}, u32[]{:S(2)}, u32[]{:S(2)}) collective-permute-start(bf16[400,128]{1,0:T(8,128)(2,1)S(1)} %get-tuple-element.78), channel_id=1, source_target_pairs={{0,64},{32,96},{64,128},{96,160},{128,192},{160,224},{192,0},{224,... | collective-permute-start | bytes 307208 | tf_op jit(solution)/shard_map/ppermute | solution.py:28
  116.0 4.0 %collective-permute-start.26 = (bf16[400,128]{1,0:T(8,128)(2,1)S(1)}, bf16[400,128]{1,0:T(8,128)(2,1)S(1)}, u32[]{:S(2)}, u32[]{:S(2)}) collective-permute-start(bf16[400,128]{1,0:T(8,128)(2,1)S(1)} %get-tuple-element.79), channel_id=1, source_target_pairs={{0,96},{32,128},{64,160},{96,192},{128,224},{160,0},{192,32},{224,... | collective-permute-start | bytes 307208 | tf_op jit(solution)/shard_map/ppermute | solution.py:28
  120.6 4.9 %collective-permute-start.28 = (bf16[400,128]{1,0:T(8,128)(2,1)S(1)}, bf16[400,128]{1,0:T(8,128)(2,1)S(1)}, u32[]{:S(2)}, u32[]{:S(2)}) collective-permute-start(bf16[400,128]{1,0:T(8,128)(2,1)S(1)} %get-tuple-element.81), channel_id=1, source_target_pairs={{0,160},{32,192},{64,224},{96,0},{128,32},{160,64},{192,96},{224,1... | collective-permute-start | bytes 307208 | tf_op jit(solution)/shard_map/ppermute | solution.py:28
  125.5 2.7 %collective-permute-start.29 = (bf16[400,128]{1,0:T(8,128)(2,1)S(1)}, bf16[400,128]{1,0:T(8,128)(2,1)S(1)}, u32[]{:S(2)}, u32[]{:S(2)}) collective-permute-start(bf16[400,128]{1,0:T(8,128)(2,1)S(1)} %get-tuple-element.82), channel_id=1, source_target_pairs={{0,192},{32,224},{64,0},{96,32},{128,64},{160,96},{192,128},{224,1... | collective-permute-start | bytes 307208 | tf_op jit(solution)/shard_map/ppermute | solution.py:28
  129.8 2.6 %collective-permute-done.26.refs_3_ = bf16[400,128]{1,0:T(8,128)(2,1)S(1)} collective-permute-done((bf16[400,128]{1,0:T(8,128)(2,1)S(1)}, bf16[400,128]{1,0:T(8,128)(2,1)S(1)}, u32[]{:S(2)}, u32[]{:S(2)}) %collective-permute-start.26) | collective-permute-done | bytes 102432 | tf_op jit(solution)/shard_map/ppermute | solution.py:28
  132.4 3.9 %collective-permute-done.28.refs_5_ = bf16[400,128]{1,0:T(8,128)(2,1)S(1)} collective-permute-done((bf16[400,128]{1,0:T(8,128)(2,1)S(1)}, bf16[400,128]{1,0:T(8,128)(2,1)S(1)}, u32[]{:S(2)}, u32[]{:S(2)}) %collective-permute-start.28) | collective-permute-done | bytes 102432 | tf_op jit(solution)/shard_map/ppermute | solution.py:28
  136.3 1.9 collective-permute-done.29.refs_6_
  141.7 26.2 %all-gather = bf16[3200,128]{1,0:T(8,128)(2,1)S(1)} all-gather(bf16[400,128]{1,0:T(8,128)(2,1)S(1)} %shard_map.148), channel_id=2, replica_groups=mesh['z'=8,'y'=4,'x'=4,'core'=2] {'z'}, dimensions={0}, use_global_device_ids=true | all-gather | bytes 921600 | tf_op jit(solution)/shard_map/all_gather | solution.py:458
  168.0 1.9 collective-permute-start.33
  170.0 16.3 %collective-permute-done.33.above = bf16[8,400,128]{2,1,0:T(8,128)(2,1)S(1)} collective-permute-done((bf16[8,400,128]{2,1,0:T(8,128)(2,1)S(1)}, bf16[8,400,128]{2,1,0:T(8,128)(2,1)S(1)}, u32[]{:S(2)}, u32[]{:S(2)}) %collective-permute-start.33) | collective-permute-done | bytes 819232 | tf_op jit(solution)/shard_map/ppermute | solution.py:28
  186.3 1.9 collective-permute-start.35
  188.5 5.8 %collective-permute-done.35.high = bf16[4,400,128]{2,1,0:T(8,128)(2,1)S(1)} collective-permute-done((bf16[4,400,128]{2,1,0:T(8,128)(2,1)S(1)}, bf16[4,400,128]{2,1,0:T(8,128)(2,1)S(1)}, u32[]{:S(2)}, u32[]{:S(2)}) %collective-permute-start.35) | collective-permute-done | bytes 409632 | tf_op jit(solution)/shard_map/ppermute | solution.py:28
  194.3 3.2 %collective-permute-done.34.low = bf16[4,400,128]{2,1,0:T(8,128)(2,1)S(1)} collective-permute-done((bf16[4,400,128]{2,1,0:T(8,128)(2,1)S(1)}, bf16[4,400,128]{2,1,0:T(8,128)(2,1)S(1)}, u32[]{:S(2)}, u32[]{:S(2)}) %collective-permute-start.34) | collective-permute-done | bytes 409632 | tf_op jit(solution)/shard_map/ppermute | solution.py:28
  197.5 2.6 %shard_map.149 = (bf16[4,8,128,128]{3,2,1,0:T(8,128)(2,1)}, bf16[4,128,1024]{2,1,0:T(8,128)(2,1)}, bf16[4,2,8,64,128]{4,3,2,1,0:T(8,128)(2,1)}, f32[1,1]{1,0:T(1...) custom-call(s32[4]{0:T(128)S(1)} %copy-done.1, bf16[8,400,128]{2,1,0:T(8,128)(2,1)S(1)} %bitcast.80, ...), custom_call_target="tpu_custom_call" | custom-call | tf_op jit(solution)/shard_map/pallas_call | solution.py:66
  (94 shorter events, 39.4 us)
Async XLA Ops:
  6.6 27.3 %collective-permute-start.10 = (bf16[3072,128]{1,0:T(8,128)(2,1)}, bf16[3072,128]{1,0:T(8,128)(2,1)S(1)}, u32[]{:S(2)}, u32[]{:S(2)}) collective-permute-start(bf16[3072,128]{1,0:T(8,128)(2,1)} %pack_kernel.1.own), channel_id=1, source_target_pairs={{0,6},{2,0},{4,2},{6,4},{1,7},{3,1},{5,3},{7,5},{8,14},{10,8},{12,... | collective-permute-start | bytes 2359304 | tf_op jit(solution)/shard_map/ppermute | solution.py:28
  7.2 28.1 %collective-permute-start.8 = (bf16[3072,128]{1,0:T(8,128)(2,1)}, bf16[3072,128]{1,0:T(8,128)(2,1)S(1)}, u32[]{:S(2)}, u32[]{:S(2)}) collective-permute-start(bf16[3072,128]{1,0:T(8,128)(2,1)} %pack_kernel.1.own), channel_id=1, source_target_pairs={{0,2},{2,4},{4,6},{6,0},{1,3},{3,5},{5,7},{7,1},{8,10},{10,12},{12... | collective-permute-start | bytes 2359304 | tf_op jit(solution)/shard_map/ppermute | solution.py:28
  9.1 8.7 %collective-permute-start.3 = (bf16[2,256,128]{2,1,0:T(8,128)(2,1)S(1)}, bf16[2,256,128]{2,1,0:T(8,128)(2,1)S(1)}, u32[]{:S(2)}, u32[]{:S(2)}) collective-permute-start(bf16[2,256,128]{2,1,0:T(8,128)(2,1)S(1)} %get-tuple-element.108), channel_id=1, source_target_pairs={{0,24},{8,0},{16,8},{24,16},{1,25},{9,1},{17,9},{25,17},{2,26},{10... | collective-permute-start | bytes 393224 | tf_op jit(solution)/shard_map/ppermute | solution.py:28
  12.2 7.9 %collective-permute-start.2 = (bf16[2,256,128]{2,1,0:T(8,128)(2,1)S(1)}, bf16[2,256,128]{2,1,0:T(8,128)(2,1)S(1)}, u32[]{:S(2)}, u32[]{:S(2)}) collective-permute-start(bf16[2,256,128]{2,1,0:T(8,128)(2,1)S(1)} %get-tuple-element.109), channel_id=1, source_target_pairs={{0,16},{8,24},{16,0},{24,8},{1,17},{9,25},{17,1},{25,9},{2,18},{10... | collective-permute-start | bytes 393224 | tf_op jit(solution)/shard_map/ppermute | solution.py:28
  12.8 8.7 %collective-permute-start.1 = (bf16[2,256,128]{2,1,0:T(8,128)(2,1)S(1)}, bf16[2,256,128]{2,1,0:T(8,128)(2,1)S(1)}, u32[]{:S(2)}, u32[]{:S(2)}) collective-permute-start(bf16[2,256,128]{2,1,0:T(8,128)(2,1)S(1)} %get-tuple-element.110), channel_id=1, source_target_pairs={{0,8},{8,16},{16,24},{24,0},{1,9},{9,17},{17,25},{25,1},{2,10},{10... | collective-permute-start | bytes 393224 | tf_op jit(solution)/shard_map/ppermute | solution.py:28
  21.7 8.5 %collective-permute-start.6 = (bf16[2,256,128]{2,1,0:T(8,128)(2,1)S(1)}, bf16[2,256,128]{2,1,0:T(8,128)(2,1)S(1)}, u32[]{:S(2)}, u32[]{:S(2)}) collective-permute-start(bf16[2,256,128]{2,1,0:T(8,128)(2,1)S(1)} %get-tuple-element.105), channel_id=1, source_target_pairs={{0,6},{2,0},{4,2},{6,4},{1,7},{3,1},{5,3},{7,5},{8,14},{10,8},{12,... | collective-permute-start | bytes 393224 | tf_op jit(solution)/shard_map/ppermute | solution.py:28
  22.3 10.1 %collective-permute-start.5 = (bf16[2,256,128]{2,1,0:T(8,128)(2,1)S(1)}, bf16[2,256,128]{2,1,0:T(8,128)(2,1)S(1)}, u32[]{:S(2)}, u32[]{:S(2)}) collective-permute-start(bf16[2,256,128]{2,1,0:T(8,128)(2,1)S(1)} %get-tuple-element.106), channel_id=1, source_target_pairs={{0,4},{2,6},{4,0},{6,2},{1,5},{3,7},{5,1},{7,3},{8,12},{10,14},{12... | collective-permute-start | bytes 393224 | tf_op jit(solution)/shard_map/ppermute | solution.py:28
  26.2 7.5 %collective-permute-start.4 = (bf16[2,256,128]{2,1,0:T(8,128)(2,1)S(1)}, bf16[2,256,128]{2,1,0:T(8,128)(2,1)S(1)}, u32[]{:S(2)}, u32[]{:S(2)}) collective-permute-start(bf16[2,256,128]{2,1,0:T(8,128)(2,1)S(1)} %get-tuple-element.107), channel_id=1, source_target_pairs={{0,2},{2,4},{4,6},{6,0},{1,3},{3,5},{5,7},{7,1},{8,10},{10,12},{12... | collective-permute-start | bytes 393224 | tf_op jit(solution)/shard_map/ppermute | solution.py:28
  33.8 2.4 %collective-permute-start.7 = (bf16[4,2,256,128]{3,2,1,0:T(8,128)(2,1)S(1)}, bf16[4,2,256,128]{3,2,1,0:T(8,128)(2,1)S(1)}, u32[]{:S(2)}, u32[]{:S(2)}) collective-permute-start(bf16[4,2,256,128]{3,2,1,0:T(8,128)(2,1)S(1)} %pad_maximum_fusion.2.near), channel_id=1, source_target_pairs={{0,1},{1,0},{2,3},{3,2},{4,5},{5,4},{6,7},{7,6},{8,9},{9,8},{10,11... | collective-permute-start | bytes 1572872 | tf_op jit(solution)/shard_map/ppermute | solution.py:32
  34.0 11.6 %collective-permute-start.11 = (bf16[1536,128]{1,0:T(8,128)(2,1)S(1)}, bf16[1536,128]{1,0:T(8,128)(2,1)S(1)}, u32[]{:S(2)}, u32[]{:S(2)}) collective-permute-start(bf16[1536,128]{1,0:T(8,128)(2,1)S(1)} %slice.69), channel_id=1, source_target_pairs={{0,6},{2,0},{4,2},{6,4},{1,7},{3,1},{5,3},{7,5},{8,14},{10,8},{12,... | collective-permute-start | bytes 1179656 | tf_op jit(solution)/shard_map/ppermute | solution.py:28
  35.4 11.8 %collective-permute-start.9 = (bf16[1536,128]{1,0:T(8,128)(2,1)S(1)}, bf16[1536,128]{1,0:T(8,128)(2,1)S(1)}, u32[]{:S(2)}, u32[]{:S(2)}) collective-permute-start(bf16[1536,128]{1,0:T(8,128)(2,1)S(1)} %slice.68), channel_id=1, source_target_pairs={{0,2},{2,4},{4,6},{6,0},{1,3},{3,5},{5,7},{7,1},{8,10},{10,12},{12... | collective-permute-start | bytes 1179656 | tf_op jit(solution)/shard_map/ppermute | solution.py:28
  49.0 9.5 %collective-permute-start.12 = (f32[256,512]{1,0:T(8,128)S(1)}, f32[256,512]{1,0:T(8,128)S(1)}, u32[]{:S(2)}, u32[]{:S(2)}) collective-permute-start(f32[256,512]{1,0:T(8,128)S(1)} %get-tuple-element.58), channel_id=1, source_target_pairs={{0,1},{1,0},{2,3},{3,2},{4,5},{5,4},{6,7},{7,6},{8,9},{9,8},{10,11... | collective-permute-start | bytes 1572872 | tf_op jit(solution)/shard_map/ppermute | solution.py:32
  49.1 9.4 %collective-permute-start.13 = (f32[4,128]{1,0:T(4,128)S(1)}, f32[4,128]{1,0:T(4,128)S(1)}, u32[]{:S(2)}, u32[]{:S(2)}) collective-permute-start(f32[4,128]{1,0:T(4,128)S(1)} %pad_maximum_fusion.3), channel_id=1, source_target_pairs={{0,0},{2,8},{4,16},{6,24},{8,2},{10,10},{12,18},{14,26},{16,4},{18... | collective-permute-start | bytes 6152 | tf_op jit(solution)/shard_map/ppermute | solution.py:49
  61.3 3.7 %collective-permute-start.17 = (f32[2,128]{1,0:T(2,128)S(1)}, f32[2,128]{1,0:T(2,128)S(1)}, u32[]{:S(2)}, u32[]{:S(2)}) collective-permute-start(f32[2,128]{1,0:T(2,128)S(1)} %shard_map.140.own), channel_id=1, source_target_pairs={{0,24},{8,0},{16,8},{24,16},{1,25},{9,1},{17,9},{25,17},{2,26},{10... | collective-permute-start | bytes 3080 | tf_op jit(solution)/shard_map/ppermute | solution.py:28
  61.4 5.2 %collective-permute-start.16 = (f32[2,128]{1,0:T(2,128)S(1)}, f32[2,128]{1,0:T(2,128)S(1)}, u32[]{:S(2)}, u32[]{:S(2)}) collective-permute-start(f32[2,128]{1,0:T(2,128)S(1)} %shard_map.140.own), channel_id=1, source_target_pairs={{0,16},{8,24},{16,0},{24,8},{1,17},{9,25},{17,1},{25,9},{2,18},{10... | collective-permute-start | bytes 3080 | tf_op jit(solution)/shard_map/ppermute | solution.py:28
  62.0 5.6 %collective-permute-start.15 = (f32[2,128]{1,0:T(2,128)S(1)}, f32[2,128]{1,0:T(2,128)S(1)}, u32[]{:S(2)}, u32[]{:S(2)}) collective-permute-start(f32[2,128]{1,0:T(2,128)S(1)} %shard_map.140.own), channel_id=1, source_target_pairs={{0,8},{8,16},{16,24},{24,0},{1,9},{9,17},{17,25},{25,1},{2,10},{10... | collective-permute-start | bytes 3080 | tf_op jit(solution)/shard_map/ppermute | solution.py:28
  71.7 16.5 %collective-permute-start.19 = (bf16[4,384,128]{2,1,0:T(8,128)(2,1)S(1)}, bf16[4,384,128]{2,1,0:T(8,128)(2,1)S(1)}, u32[]{:S(2)}, u32[]{:S(2)}) collective-permute-start(bf16[4,384,128]{2,1,0:T(8,128)(2,1)S(1)} %get-tuple-element.70), channel_id=1, source_target_pairs={{0,2},{2,4},{4,6},{6,0},{1,3},{3,5},{5,7},{7,1},{8,10},{10,12},{12... | collective-permute-start | bytes 1179656 | tf_op jit(solution)/shard_map/ppermute | solution.py:28
  74.7 13.5 %collective-permute-start.20 = (bf16[4,384,128]{2,1,0:T(8,128)(2,1)S(1)}, bf16[4,384,128]{2,1,0:T(8,128)(2,1)S(1)}, u32[]{:S(2)}, u32[]{:S(2)}) collective-permute-start(bf16[4,384,128]{2,1,0:T(8,128)(2,1)S(1)} %get-tuple-element.71), channel_id=1, source_target_pairs={{0,6},{2,0},{4,2},{6,4},{1,7},{3,1},{5,3},{7,5},{8,14},{10,8},{12,... | collective-permute-start | bytes 1179656 | tf_op jit(solution)/shard_map/ppermute | solution.py:28
  75.5 12.0 %collective-permute-start.21 = (f32[2,128]{1,0:T(2,128)S(1)}, f32[2,128]{1,0:T(2,128)S(1)}, u32[]{:S(2)}, u32[]{:S(2)}) collective-permute-start(f32[2,128]{1,0:T(2,128)S(1)} %get-tuple-element.73), channel_id=1, source_target_pairs={{0,0},{2,8},{4,16},{6,24},{8,2},{10,10},{12,18},{14,26},{16,4},{18... | collective-permute-start | bytes 3080 | tf_op jit(solution)/shard_map/ppermute | solution.py:49
  89.6 18.5 %collective-permute-start.22 = (bf16[8,384,128]{2,1,0:T(8,128)(2,1)S(1)}, bf16[8,384,128]{2,1,0:T(8,128)(2,1)S(1)}, u32[]{:S(2)}, u32[]{:S(2)}) collective-permute-start(bf16[8,384,128]{2,1,0:T(8,128)(2,1)S(1)} %get-tuple-element.74), channel_id=1, source_target_pairs={{0,2},{2,4},{4,6},{6,0},{1,3},{3,5},{5,7},{7,1},{8,10},{10,12},{12... | collective-permute-start | bytes 2359304 | tf_op jit(solution)/shard_map/ppermute | solution.py:28
  92.0 17.9 %collective-permute-start.23 = (bf16[8,384,128]{2,1,0:T(8,128)(2,1)S(1)}, bf16[8,384,128]{2,1,0:T(8,128)(2,1)S(1)}, u32[]{:S(2)}, u32[]{:S(2)}) collective-permute-start(bf16[8,384,128]{2,1,0:T(8,128)(2,1)S(1)} %get-tuple-element.75), channel_id=1, source_target_pairs={{0,6},{2,0},{4,2},{6,4},{1,7},{3,1},{5,3},{7,5},{8,14},{10,8},{12,... | collective-permute-start | bytes 2359304 | tf_op jit(solution)/shard_map/ppermute | solution.py:28
  110.7 14.8 %collective-permute-start.24 = (bf16[400,128]{1,0:T(8,128)(2,1)S(1)}, bf16[400,128]{1,0:T(8,128)(2,1)S(1)}, u32[]{:S(2)}, u32[]{:S(2)}) collective-permute-start(bf16[400,128]{1,0:T(8,128)(2,1)S(1)} %get-tuple-element.77), channel_id=1, source_target_pairs={{0,32},{32,64},{64,96},{96,128},{128,160},{160,192},{192,224},{224... | collective-permute-start | bytes 307208 | tf_op jit(solution)/shard_map/ppermute | solution.py:28
  112.7 17.0 %collective-permute-start.25 = (bf16[400,128]{1,0:T(8,128)(2,1)S(1)}, bf16[400,128]{1,0:T(8,128)(2,1)S(1)}, u32[]{:S(2)}, u32[]{:S(2)}) collective-permute-start(bf16[400,128]{1,0:T(8,128)(2,1)S(1)} %get-tuple-element.78), channel_id=1, source_target_pairs={{0,64},{32,96},{64,128},{96,160},{128,192},{160,224},{192,0},{224,... | collective-permute-start | bytes 307208 | tf_op jit(solution)/shard_map/ppermute | solution.py:28
  116.0 16.4 %collective-permute-start.26 = (bf16[400,128]{1,0:T(8,128)(2,1)S(1)}, bf16[400,128]{1,0:T(8,128)(2,1)S(1)}, u32[]{:S(2)}, u32[]{:S(2)}) collective-permute-start(bf16[400,128]{1,0:T(8,128)(2,1)S(1)} %get-tuple-element.79), channel_id=1, source_target_pairs={{0,96},{32,128},{64,160},{96,192},{128,224},{160,0},{192,32},{224,... | collective-permute-start | bytes 307208 | tf_op jit(solution)/shard_map/ppermute | solution.py:28
  120.0 12.4 %collective-permute-start.27 = (bf16[400,128]{1,0:T(8,128)(2,1)S(1)}, bf16[400,128]{1,0:T(8,128)(2,1)S(1)}, u32[]{:S(2)}, u32[]{:S(2)}) collective-permute-start(bf16[400,128]{1,0:T(8,128)(2,1)S(1)} %get-tuple-element.80), channel_id=1, source_target_pairs={{0,128},{32,160},{64,192},{96,224},{128,0},{160,32},{192,64},{224,... | collective-permute-start | bytes 307208 | tf_op jit(solution)/shard_map/ppermute | solution.py:28
  120.6 15.7 %collective-permute-start.28 = (bf16[400,128]{1,0:T(8,128)(2,1)S(1)}, bf16[400,128]{1,0:T(8,128)(2,1)S(1)}, u32[]{:S(2)}, u32[]{:S(2)}) collective-permute-start(bf16[400,128]{1,0:T(8,128)(2,1)S(1)} %get-tuple-element.81), channel_id=1, source_target_pairs={{0,160},{32,192},{64,224},{96,0},{128,32},{160,64},{192,96},{224,1... | collective-permute-start | bytes 307208 | tf_op jit(solution)/shard_map/ppermute | solution.py:28
  125.5 12.6 %collective-permute-start.29 = (bf16[400,128]{1,0:T(8,128)(2,1)S(1)}, bf16[400,128]{1,0:T(8,128)(2,1)S(1)}, u32[]{:S(2)}, u32[]{:S(2)}) collective-permute-start(bf16[400,128]{1,0:T(8,128)(2,1)S(1)} %get-tuple-element.82), channel_id=1, source_target_pairs={{0,192},{32,224},{64,0},{96,32},{128,64},{160,96},{192,128},{224,1... | collective-permute-start | bytes 307208 | tf_op jit(solution)/shard_map/ppermute | solution.py:28
  129.8 9.5 %collective-permute-start.30 = (bf16[400,128]{1,0:T(8,128)(2,1)S(1)}, bf16[400,128]{1,0:T(8,128)(2,1)S(1)}, u32[]{:S(2)}, u32[]{:S(2)}) collective-permute-start(bf16[400,128]{1,0:T(8,128)(2,1)S(1)} %get-tuple-element.83), channel_id=1, source_target_pairs={{0,224},{32,0},{64,32},{96,64},{128,96},{160,128},{192,160},{224,1... | collective-permute-start | bytes 307208 | tf_op jit(solution)/shard_map/ppermute | solution.py:28
  168.0 18.3 %collective-permute-start.33 = (bf16[8,400,128]{2,1,0:T(8,128)(2,1)S(1)}, bf16[8,400,128]{2,1,0:T(8,128)(2,1)S(1)}, u32[]{:S(2)}, u32[]{:S(2)}) collective-permute-start(bf16[8,400,128]{2,1,0:T(8,128)(2,1)S(1)} %bitcast.78), channel_id=1, source_target_pairs={{0,24},{8,0},{16,8},{24,16},{1,25},{9,1},{17,9},{25,17},{2,26},{10... | collective-permute-start | bytes 2457608 | tf_op jit(solution)/shard_map/ppermute | solution.py:28
  169.8 18.4 %collective-permute-start.32 = (bf16[8,400,128]{2,1,0:T(8,128)(2,1)S(1)}, bf16[8,400,128]{2,1,0:T(8,128)(2,1)S(1)}, u32[]{:S(2)}, u32[]{:S(2)}) collective-permute-start(bf16[8,400,128]{2,1,0:T(8,128)(2,1)S(1)} %bitcast.79), channel_id=1, source_target_pairs={{0,8},{8,16},{16,24},{24,0},{1,9},{9,17},{17,25},{25,1},{2,10},{10... | collective-permute-start | bytes 2457608 | tf_op jit(solution)/shard_map/ppermute | solution.py:28
  186.3 8.0 %collective-permute-start.35 = (bf16[4,400,128]{2,1,0:T(8,128)(2,1)S(1)}, bf16[4,400,128]{2,1,0:T(8,128)(2,1)S(1)}, u32[]{:S(2)}, u32[]{:S(2)}) collective-permute-start(bf16[4,400,128]{2,1,0:T(8,128)(2,1)S(1)} %slice.71), channel_id=1, source_target_pairs={{0,24},{8,0},{16,8},{24,16},{1,25},{9,1},{17,9},{25,17},{2,26},{10... | collective-permute-start | bytes 1228808 | tf_op jit(solution)/shard_map/ppermute | solution.py:28
  188.3 9.2 %collective-permute-start.34 = (bf16[4,400,128]{2,1,0:T(8,128)(2,1)S(1)}, bf16[4,400,128]{2,1,0:T(8,128)(2,1)S(1)}, u32[]{:S(2)}, u32[]{:S(2)}) collective-permute-start(bf16[4,400,128]{2,1,0:T(8,128)(2,1)S(1)} %slice.70), channel_id=1, source_target_pairs={{0,8},{8,16},{16,24},{24,0},{1,9},{9,17},{17,25},{25,1},{2,10},{10... | collective-permute-start | bytes 1228808 | tf_op jit(solution)/shard_map/ppermute | solution.py:28
  (12 other events, 33.7 us)
